TPU v7x, 128 devices: a whole 4x4x4 slice. The times are simulated.
128 devices in a mesh: coarse: 2 (over z_hi), fine: 8 (over z_lo, y), model: 8 (over x, core).
Axes of the slice: x: 4, y: 4, z: 4 (z_hi: 2, z_lo: 2; z = z_hi * 2 + z_lo), core: 2. Of those that a mesh axis runs over, the one named last changes fastest.
Arguments:
- fresh_keys: bfloat16 [16, 24576, 8, 128], P(None, ('coarse', 'fine'), 'model'), may hold values from -6 to 6
- fresh_values: bfloat16 [16, 24576, 8, 128], P(None, ('coarse', 'fine'), 'model'), may hold values from -6 to 6
- turn_angle: float32 [24576, 64], replicated, may hold values from -3.140625 to 3.140625
Outputs:
- cache_keys: bfloat16 [16, 24576, 8, 128], P(('coarse', 'fine'), None, 'model')
- cache_values: bfloat16 [16, 24576, 8, 128], P(('coarse', 'fine'), None, 'model')
- page_high: bfloat16 [16, 768, 8, 128], P(('coarse', 'fine'), None, 'model')
- page_low: bfloat16 [16, 768, 8, 128], P(('coarse', 'fine'), None, 'model')
All inputs are finite; a program needn't handle non-finite values.
Results may differ from a plain program's by a relative error of at most 0.001.
Values may be sent and summed in bfloat16 or wider, within the bound.
No kernel may reach another device: no remote copies, remote signals or barrier semaphores. Data moves between devices by JAX's collectives and lax.ppermute only.
A program may use at most 128 MiB of HBM per device.

v0:
```python
import jax
import jax.numpy as jnp
from jax import lax
from jax.sharding import PartitionSpec as P

PAGE = 32


def in_one_piece(arrays, axis, split_dim, concat_dim, along):
    ends, at = ([], 0)
    for a in arrays[:-1]:
        at += a.shape[along]
        ends.append(at)
    both = jnp.concatenate(arrays, axis=along)
    return tuple(
        jnp.split(
            lax.all_to_all(both, axis, split_axis=split_dim, concat_axis=concat_dim, tiled=True),
            ends,
            axis=along,
        )
    )


def turn_pairs(vectors, angle):
    half = vectors.shape[-1] // 2
    cosine, sine = (jnp.cos(angle)[None, :, None, :], jnp.sin(angle)[None, :, None, :])
    first, second = (vectors[..., :half], vectors[..., half:])
    return jnp.concatenate(
        [first * cosine - second * sine, second * cosine + first * sine], axis=-1
    )


def prepare_keys(plain_keys, angle):
    wide_keys = plain_keys.astype(jnp.float32)
    return turn_pairs(wide_keys, angle)


def on_device(fresh_keys, fresh_values, turn_angle):
    my_angles = lax.dynamic_slice_in_dim(
        turn_angle, lax.axis_index(("coarse", "fine")) * fresh_keys.shape[1], fresh_keys.shape[1]
    )
    sent_keys = prepare_keys(fresh_keys, my_angles).astype(jnp.bfloat16)
    moved_keys, cache_values = in_one_piece((sent_keys, fresh_values), ("coarse", "fine"), 0, 1, 2)
    page_view = moved_keys.reshape(
        moved_keys.shape[0], -1, PAGE, moved_keys.shape[2], moved_keys.shape[3]
    )
    page_high = jnp.max(page_view, axis=2)
    page_low = jnp.min(page_view, axis=2)
    return (moved_keys, cache_values, page_high, page_low)


def solution(mesh):
    return jax.shard_map(
        on_device,
        mesh=mesh,
        in_specs=(
            P(None, ("coarse", "fine"), "model", None),
            P(None, ("coarse", "fine"), "model", None),
            P(),
        ),
        out_specs=(
            P(("coarse", "fine"), None, "model", None),
            P(("coarse", "fine"), None, "model", None),
            P(("coarse", "fine"), None, "model", None),
            P(("coarse", "fine"), None, "model", None),
        ),
        check_vma=False,
    )
```

profile of v0, /device:TPU:0, one launch (start us, length us, event | category | flops | bytes accessed | tf_op | source)
XLA Modules:
  0.0 182.6 jit_solution(2764367730118668713)
XLA Ops:
  0.6 2.3 %dynamic-slice_cosine_fusion = (f32[1536,64]{0,1:T(8,128)S(1)}, f32[1536,64]{0,1:T(8,128)S(1)}) fusion(f32[24576,64]{0,1:T(8,128)} %param.5, s32[]{:T(128)S(6)} %select_n.3), kind=kLoop, calls=%fused_computation.4 | loop fusion | bytes 1179652 | tf_op jit(solution)/shard_map/cos | solution.py:26
  3.0 1.2 copy.7
  4.1 1.2 copy.8
  5.3 4.0 %convert_element_type.12 = f32[16,1536,1,128]{3,1,2,0:T(8,128)S(1)} convert(bf16[16,1536,1,128]{3,1,2,0:T(8,128)(2,1)} %param.3) | non-fusion elementwise | flops 3145728 | bytes 18874368 | tf_op jit(solution)/shard_map/convert_element_type | solution.py:34
  9.3 5.5 %subtract_convert_fusion = (bf16[16,1536,1,64]{3,1,2,0:T(8,128)(2,1)S(1)}, bf16[16,1536,1,64]{3,1,2,0:T(8,128)(2,1)S(1)}) fusion(f32[16,1536,1,128]{3,1,2,0:T(8,128)S(1)} %convert_element_type.12, f32[1536,64]{1,0:T(8,128)} %copy.8, f32[1536,64]{1,0:T(8,128)} %copy.7), kind=kLoop, calls=%fused_computation.2 | loop fusion | flops 12582912 | bytes 19660800 | tf_op jit(solution)/shard_map/convert
  14.9 6.4 %pad_maximum_fusion = bf16[16,1536,2,128]{3,1,2,0:T(8,128)(2,1)S(1)} fusion(bf16[16,1536,1,128]{3,1,2,0:T(8,128)(2,1)} %param.4, bf16[16,1536,1,64]{3,1,2,0:T(8,128)(2,1)S(1)} %get-tuple-element.7, bf16[16,1536,1,64]{3,1,2,0:T(8,128)(2,1)S(1)} %get-tuple-element.6), kind=kLoop, calls=%fused_computation | loop fusion | flops 37748736 | bytes 25165824 | tf_op jit(solution)/shard_map/concatenate | solution.py:14
  21.3 148.7 %all_to_all.12 = bf16[16,1536,2,128]{3,1,2,0:T(8,128)(2,1)S(1)} all-to-all(bf16[16,1536,2,128]{3,1,2,0:T(8,128)(2,1)S(1)} %pad_maximum_fusion), channel_id=1, replica_groups=mesh['coarse'=2,'fine'=8,'model'=8] {'coarse','fine'}, dimensions={0} | all-to-all | bytes 25165824 | tf_op jit(solution)/shard_map/all_to_all | solution.py:17
  170.0 1.9 %copy.9 = bf16[16,1536,2,128]{3,1,0,2:T(8,128)(2,1)S(1)} copy(bf16[16,1536,2,128]{3,1,2,0:T(8,128)(2,1)S(1)} %all_to_all.12) | data formatting | bytes 25165824 | tf_op jit(solution)/shard_map/all_to_all | solution.py:17
  171.9 3.2 %fusion.1 = (bf16[1,24576,1,128]{3,1,2,0:T(8,128)(2,1)}, bf16[1,24576,1,128]{3,1,2,0:T(8,128)(2,1)S(1)}) fusion(bf16[1,24576,2,128]{3,1,2,0:T(8,128)(2,1)S(1)} %bitcast.4), kind=kLoop, calls=%fused_computation.6 | loop fusion | bytes 25165824 | tf_op jit(solution)/shard_map/split | solution.py:16
  175.2 0.0 copy-start
  175.2 7.5 %fusion = (bf16[768,128]{1,0:T(8,128)(2,1)}, bf16[768,128]{1,0:T(8,128)(2,1)}) fusion(bf16[1,768,32,1,128]{4,2,1,3,0:T(8,128)(2,1)S(1)} %bitcast.5), kind=kLoop, calls=%fused_computation.5 | loop fusion | flops 6094848 | bytes 6684672 | tf_op jit(solution)/shard_map/reduce_min | solution.py:48
  182.6 0.0 copy-done
Async XLA Ops:
  175.2 7.5 %copy-start = (bf16[1,24576,1,128]{3,1,2,0:T(8,128)(2,1)}, bf16[1,24576,1,128]{3,1,2,0:T(8,128)(2,1)S(1)}, u32[]{:S(2)}) copy-start(bf16[1,24576,1,128]{3,1,2,0:T(8,128)(2,1)S(1)} %get-tuple-element.9) | copy-start | bytes 18874372
where the time goes:
time: 183 us
  blocking collectives  149 us (81%)
  other arithmetic  23.5 us (13%)
  local copies, waits for them, and re-layouts  9.78 us (5%)
    all_to_all x1, blocking collectives, in_one_piece(): lax.all_to_all(both, axis, split_axis=split_dim, concat_axis=concat_dim,...  149 us
    reduce_min x1, other arithmetic, on_device(): page_low = jnp.min(page_view, axis=2)  7.47 us
    concatenate x1, other arithmetic, in_one_piece(): both = jnp.concatenate(arrays, axis=along)  6.43 us
    another operation x1, other arithmetic  5.51 us
    convert_element_type x1, other arithmetic, prepare_keys(): wide_keys = plain_keys.astype(jnp.float32)  4.04 us

commit v1 on v0

v1 whole, which is shorter than its diff:
```python
import functools

import jax
import jax.numpy as jnp
from jax import lax
from jax.experimental import pallas as pl
from jax.experimental.pallas import tpu as pltpu
from jax.sharding import PartitionSpec as P

PAGE = 32
SEQ = ("coarse", "fine")
ROWS = 16
ANY = pl.BlockSpec(memory_space=pl.ANY)


def cos_sin(a):
    j = jnp.floor(a * 0.636619772367581 + 0.5)
    r = a - j * 1.5703125
    r = r - j * 4.837512969970703e-4
    r = r - j * 7.549789948768648e-8
    z = r * r
    s = r + r * z * (-1.6666654611e-1 + z * (8.3321608736e-3 + z * -1.9515295891e-4))
    c = 1.0 - 0.5 * z + z * z * (4.166664568298827e-2 + z * (-1.388731625493765e-3 + z * 2.443315711809948e-5))
    odd = jnp.abs(j) == 1.0
    near_c = jnp.where(odd, s, c)
    near_s = jnp.where(odd, c, s)
    cosine = jnp.where(j == 0.0, near_c, jnp.where(j == -1.0, near_c, -near_c))
    sine = jnp.where(j == 0.0, near_s, jnp.where(j == 1.0, near_s, -near_s))
    return cosine, sine


def head_kernel(shards, keys, values, angles, out, raw, turn, wide_c, wide_s, key_sem, value_sem, angle_sem):
    seqs, n, _ = keys.shape
    half = turn.shape[0]
    me = lax.axis_index("coarse") * shards + lax.axis_index("fine")
    angle_in = pltpu.make_async_copy(angles.at[:, pl.ds(pl.multiple_of(me * n, n), n)], turn, angle_sem)
    angle_in.start()
    key_in = [pltpu.make_async_copy(keys.at[b], raw.at[b], key_sem.at[b]) for b in range(seqs)]
    value_in = [pltpu.make_async_copy(values.at[b], out.at[b, 1], value_sem.at[b]) for b in range(seqs)]
    for copy in key_in + value_in:
        copy.start()
    angle_in.wait()

    def spread(t, _):
        at = pl.multiple_of(t * 128, 128)
        c, s = cos_sin(turn[:, pl.ds(at, 128)])
        wide_c[pl.ds(at, 128), :] = jnp.concatenate([c, c], axis=0).T
        wide_s[pl.ds(at, 128), :] = jnp.concatenate([-s, s], axis=0).T
        return 0

    lax.fori_loop(0, n // 128, spread, 0)
    group = 4
    for first in range(0, seqs, group):
        for b in range(first, first + group):
            key_in[b].wait()

        def rows(t, _):
            at = pl.ds(pl.multiple_of(t * ROWS, ROWS), ROWS)
            c, s = wide_c[at, :], wide_s[at, :]
            for b in range(first, first + group):
                x = raw[b, at, :].astype(jnp.float32)
                out[b, 0, at, :] = (x * c + pltpu.roll(x, half, 1) * s).astype(jnp.bfloat16)
            return 0

        lax.fori_loop(0, n // ROWS, rows, 0, unroll=2)
    for copy in value_in:
        copy.wait()


def head(keys, values, angles, shards):
    seqs, n, size = keys.shape
    f32 = jnp.float32
    return pl.pallas_call(
        functools.partial(head_kernel, shards),
        out_shape=pltpu.VMEM((seqs, 2, n, size), jnp.bfloat16),
        in_specs=[ANY] * 3,
        out_specs=pl.BlockSpec(memory_space=pltpu.VMEM),
        scratch_shapes=[
            pltpu.VMEM((seqs, n, size), jnp.bfloat16),
            pltpu.VMEM((size // 2, n), f32),
            pltpu.VMEM((n, size), f32),
            pltpu.VMEM((n, size), f32),
            pltpu.SemaphoreType.DMA((seqs,)),
            pltpu.SemaphoreType.DMA((seqs,)),
            pltpu.SemaphoreType.DMA,
        ],
        compiler_params=pltpu.CompilerParams(vmem_limit_bytes=30 << 20),
        name="head",
    )(*[pltpu.with_memory_space_constraint(a, pltpu.HBM) for a in (keys, values, angles)])


def tail_kernel(moved, keys, values, high, low, sem):
    d, _, n, _ = moved.shape
    copies = []
    for b in range(d):
        copies.append(pltpu.make_async_copy(moved.at[b, 0], keys.at[pl.ds(b * n, n)], sem.at[0, b]))
        copies.append(pltpu.make_async_copy(moved.at[b, 1], values.at[pl.ds(b * n, n)], sem.at[1, b]))
    for copy in copies:
        copy.start()
    pages = 16
    per = n // (pages * PAGE)

    def reduce(t, _):
        b, q = t // per, t % per
        rows = moved[b, 0, pl.ds(pl.multiple_of(q * pages * PAGE, pages * PAGE), pages * PAGE), :]
        rows = rows.reshape(pages, PAGE, rows.shape[-1])
        at = pl.ds(pl.multiple_of(t * pages, pages), pages)
        high[at, :] = jnp.max(rows, axis=1)
        low[at, :] = jnp.min(rows, axis=1)
        return 0

    lax.fori_loop(0, d * per, reduce, 0)
    for copy in copies:
        copy.wait()


def tail(moved):
    d, _, n, size = moved.shape
    bf16 = jnp.bfloat16
    return pl.pallas_call(
        tail_kernel,
        out_shape=[
            jax.ShapeDtypeStruct((d * n, size), bf16),
            jax.ShapeDtypeStruct((d * n, size), bf16),
            jax.ShapeDtypeStruct((d * n // PAGE, size), bf16),
            jax.ShapeDtypeStruct((d * n // PAGE, size), bf16),
        ],
        in_specs=[pl.BlockSpec(memory_space=pltpu.VMEM)],
        out_specs=[ANY, ANY, pl.BlockSpec(memory_space=pltpu.VMEM), pl.BlockSpec(memory_space=pltpu.VMEM)],
        scratch_shapes=[pltpu.SemaphoreType.DMA((2, d))],
        compiler_params=pltpu.CompilerParams(vmem_limit_bytes=16 << 20),
        name="tail",
    )(pltpu.with_memory_space_constraint(moved, pltpu.VMEM))


def solution(mesh):
    shards = mesh.shape["fine"]

    def on_device(fresh_keys, fresh_values, turn_angle):
        sent = head(fresh_keys[:, :, 0], fresh_values[:, :, 0], turn_angle.T, shards)
        moved = lax.all_to_all(sent, SEQ, split_axis=0, concat_axis=0, tiled=True)
        keys, values, high, low = tail(moved)
        return tuple(a[None, :, None] for a in (keys, values, high, low))

    cut = P(None, SEQ, "model", None)
    out = P(SEQ, None, "model", None)
    return jax.shard_map(
        on_device, mesh=mesh, in_specs=(cut, cut, P()), out_specs=(out,) * 4, check_vma=False
    )
```

time: 183 us -> 177 us (0.967)
  Pallas kernels: 0 us -> 28 us
  other arithmetic: 23.5 us -> 0 us
  local copies, waits for them, and re-layouts: 9.78 us -> 0 us
    pallas_call x0 -> x2, Pallas kernels: none -> 28 us  [the longest x1 22.4 us: head(): pl.pallas_call(functools.partial(head_kernel, shards), out_shape=pltpu.VM...]
    reduce_min x1 -> x0, other arithmetic: 7.47 us -> none  [on_device(): page_low = jnp.min(page_view, axis=2)]
    concatenate x1 -> x0, other arithmetic: 6.43 us -> none  [in_one_piece(): both = jnp.concatenate(arrays, axis=along)]
    another operation x1 -> x0, other arithmetic: 5.51 us -> none
    convert_element_type x1 -> x0, other arithmetic: 4.04 us -> none  [prepare_keys(): wide_keys = plain_keys.astype(jnp.float32)]
    cos x2 -> x0, local copies, waits for them, and re-layouts: 3.49 us -> none  [turn_pairs(): jnp.cos(angle)[None, :, None, :]]
    split x1 -> x0, local copies, waits for them, and re-layouts: 3.2 us -> none  [in_one_piece(): jnp.split(lax.all_to_all(both, axis, split_axis=split_dim, concat_axis=co...]
    all_to_all x1 -> x0, local copies, waits for them, and re-layouts: 1.94 us -> none  [in_one_piece(): lax.all_to_all(both, axis, split_axis=split_dim, concat_axis=concat_dim,...]
where the time goes in v1:
time: 177 us
  blocking collectives  149 us (84%)
  Pallas kernels  28 us (16%)
    all_to_all x1, blocking collectives, on_device(): moved = lax.all_to_all(sent, SEQ, split_axis=0, concat_axis=0, tiled=True)  149 us
    pallas_call x1, Pallas kernels, head(): pl.pallas_call(functools.partial(head_kernel, shards), out_shape=pltpu.VM...  22.4 us
    pallas_call x1, Pallas kernels, tail(): pl.pallas_call(tail_kernel, out_shape=[jax.ShapeDtypeStruct((d * n, size)...  5.55 us

profile of v1, /device:TPU:0, one launch (start us, length us, event | category | flops | bytes accessed | tf_op | source)
XLA Modules:
  0.0 177.3 jit_solution(16200382032910091482)
XLA Ops:
  0.6 22.4 %head.1 = bf16[16,2,1536,128]{3,2,1,0:T(8,128)(2,1)S(1)} custom-call(bf16[16,1536,128]{2,1,0:T(8,128)(2,1)} %bitcast.7, bf16[16,1536,128]{2,1,0:T(8,128)(2,1)} %bitcast.8, f32[64,24576]{1,0:T(8,128)} %bitcast.9), custom_call_target="tpu_custom_call" | custom-call | tf_op jit(solution)/shard_map/head/pallas_call | solution.py:73
  23.1 148.7 %all_to_all.5.moved = bf16[16,2,1536,128]{3,2,1,0:T(8,128)(2,1)S(1)} all-to-all(bf16[16,2,1536,128]{3,2,1,0:T(8,128)(2,1)S(1)} %head.1), channel_id=1, replica_groups=mesh['coarse'=2,'fine'=8,'model'=8] {'coarse','fine'}, dimensions={0} | all-to-all | bytes 25165824 | tf_op jit(solution)/shard_map/all_to_all | solution.py:141
  171.8 5.5 %tail.1 = (bf16[24576,128]{1,0:T(8,128)(2,1)}, bf16[24576,128]{1,0:T(8,128)(2,1)}, bf16[768,128]{1,0:T(8,128)(2,1)}, bf16[768,128]{1,0:T(8,128)(2,1)}) custom-call(bf16[16,2,1536,128]{3,2,1,0:T(8,128)(2,1)S(1)} %all_to_all.5.moved), custom_call_target="tpu_custom_call" | custom-call | tf_op jit(solution)/shard_map/tail/pallas_call | solution.py:120

commit v2 on v0

v2 whole, which is shorter than its diff:
```python
import functools
from typing import Any, NamedTuple

import jax
import jax.numpy as jnp
from jax import lax
from jax.experimental import pallas as pl
from jax.experimental.pallas import tpu as pltpu
from jax.sharding import PartitionSpec as P

PAGE = 32
SEQ = ("coarse", "fine")
SIDE = 4
COST = 50_000_000
ROWS = 32
UNROLL = 2
BF16 = jnp.bfloat16
VMEM_LIMIT = 20 << 20


def place():
    me = lax.axis_index("coarse") * lax.axis_size("fine") + lax.axis_index("fine")
    return me % SIDE, me // SIDE


def slot(y, z):
    return (z + 2 * SIDE) % SIDE * SIDE + (y + 2 * SIDE) % SIDE


def shift(a, dy, dz):
    pairs = [(i, slot(i % SIDE + dy, i // SIDE + dz)) for i in range(SIDE * SIDE)]
    return lax.ppermute(a, SEQ, pairs)


def cos_sin(a):
    j = jnp.floor(a * 0.636619772367581 + 0.5)
    r = a - j * 1.5703125
    r = r - j * 4.837512969970703e-4
    r = r - j * 7.549789948768648e-8
    z = r * r
    s = r + r * z * (-1.6666654611e-1 + z * (8.3321608736e-3 + z * -1.9515295891e-4))
    c = 1.0 - 0.5 * z + z * z * (4.166664568298827e-2 + z * (-1.388731625493765e-3 + z * 2.443315711809948e-5))
    odd = jnp.abs(j) == 1.0
    near_c = jnp.where(odd, s, c)
    near_s = jnp.where(odd, c, s)
    cosine = jnp.where(j == 0.0, near_c, jnp.where(j == -1.0, near_c, -near_c))
    sine = jnp.where(j == 0.0, near_s, jnp.where(j == 1.0, near_s, -near_s))
    return cosine, sine


class Task(NamedTuple):
    read: int
    block: Any
    to: int
    index: Any
    turn: Any = None
    rows: bool = False
    pages: bool = False


def value_at(index, y, z):
    return index(y, z) if callable(index) else index


def step_kernel(far, near, writes, skip, tasks, turns, *refs):
    inputs, refs = refs[: far + near], refs[far + near :]
    if turns:
        angles, refs = refs[0], refs[1:]
    outs, refs = refs[skip : skip + writes], refs[skip + writes :]
    held, turned, high, low, raw_angle, wide_c, wide_s, in_sem, out_sem, page_sem, angle_sem = refs
    n, size = held.shape[1:]
    y, z = place()
    angle_loads, loads, ready, stores = [], {}, {}, []
    h = 0
    for t, e in enumerate(turns):
        first = pl.multiple_of(slot(y - e, z) * n, n)
        angle_loads.append(pltpu.make_async_copy(angles.at[:, pl.ds(first, n)], raw_angle.at[t], angle_sem.at[t]))
    for k, task in enumerate(tasks):
        source = inputs[task.read].at[value_at(task.block, y, z)]
        if task.read >= far:
            ready[k] = source
            continue
        direct = task.turn is None and not task.rows
        if direct:
            ready[k] = outs[task.to].at[task.index]
        else:
            ready[k] = held.at[h]
            h += 1
        loads[k] = pltpu.make_async_copy(source, ready[k], in_sem.at[len(loads)])
    for load in angle_loads + list(loads.values()):
        load.start()
    for t in range(len(turns)):
        angle_loads[t].wait()

        def spread(q, _, t=t):
            lanes = pl.ds(pl.multiple_of(q * 128, 128), 128)
            c, s = cos_sin(raw_angle[t, :, lanes])
            wide_c[t, lanes, :] = jnp.concatenate([c, c], axis=0).T
            wide_s[t, lanes, :] = jnp.concatenate([-s, s], axis=0).T
            return 0

        lax.fori_loop(0, n // 128, spread, 0)
    m = p = 0
    target = {}
    for t, e in enumerate(turns):
        group = [k for k, task in enumerate(tasks) if task.turn == e]
        for k in group:
            if tasks[k].rows:
                target[k] = turned.at[m]
                m += 1
            else:
                target[k] = outs[tasks[k].to].at[tasks[k].index]
            if k in loads:
                loads.pop(k).wait()

        def rotate(q, _, t=t, group=group):
            r = pl.ds(pl.multiple_of(q * ROWS, ROWS), ROWS)
            c, s = wide_c[t, r, :], wide_s[t, r, :]
            x = [ready[k][r, :].astype(jnp.float32) for k in group]
            w = [pltpu.roll(v, size // 2, 1) for v in x]
            for k, v, u in zip(group, x, w):
                target[k][r, :] = (v * c + u * s).astype(BF16)
            return 0

        lax.fori_loop(0, n // ROWS, rotate, 0, unroll=UNROLL)
    for k, task in enumerate(tasks):
        if k in loads:
            loads[k].wait()
        block = ready[k]
        if task.turn is not None:
            block = target[k]
        elif not task.rows and k not in loads:
            to = outs[task.to].at[task.index]

            def copy(q, _, block=block, to=to):
                r = pl.ds(pl.multiple_of(q * 256, 256), 256)
                to[r, :] = block[r, :]
                return 0

            lax.fori_loop(0, n // 256, copy, 0)
        if not task.rows:
            continue
        index = value_at(task.index, y, z)
        to = outs[task.to].at[pl.ds(pl.multiple_of(index * n, n), n)]
        stores.append(pltpu.make_async_copy(block, to, out_sem.at[k]))
        stores[-1].start()
        if task.pages:
            count, group = n // PAGE, 16

            def bound(q, _, block=block, p=p):
                rows = block[pl.ds(pl.multiple_of(q * group * PAGE, group * PAGE), group * PAGE), :]
                rows = rows.reshape(group, PAGE, size)
                r = pl.ds(pl.multiple_of(q * group, group), group)
                high[p, r, :] = jnp.max(rows, axis=1)
                low[p, r, :] = jnp.min(rows, axis=1)
                return 0

            lax.fori_loop(0, count // group, bound, 0)
            for i, side in enumerate((high, low)):
                to = outs[writes - 2 + i].at[pl.ds(pl.multiple_of(index * count, 16), count)]
                stores.append(pltpu.make_async_copy(side.at[p], to, page_sem.at[i, p]))
                stores[-1].start()
            p += 1
    for store in stores:
        store.wait()


def step(far, near, angles, sent, grown, tasks):
    n, size = (*far, *near)[0].shape[-2:]
    turns = sorted({t.turn for t in tasks if t.turn is not None})
    hbm, vmem = pl.BlockSpec(memory_space=pl.ANY), pl.BlockSpec(memory_space=pltpu.VMEM)
    operands = [pltpu.with_memory_space_constraint(a, pltpu.HBM) for a in far]
    operands += [pltpu.with_memory_space_constraint(a, pltpu.VMEM) for a in near]
    in_specs = [hbm] * len(far) + [vmem] * len(near)
    if turns:
        operands.append(pltpu.with_memory_space_constraint(angles, pltpu.HBM))
        in_specs.append(hbm)
    out = [pltpu.VMEM((c, n, size), BF16) for c in sent]
    out_specs = [vmem] * len(sent) + [hbm] * len(grown)
    aliases = {}
    for a in grown:
        if hasattr(a, "dtype"):
            aliases[len(operands)] = len(out)
            operands.append(a)
            in_specs.append(hbm)
            a = a.shape
        out.append(jax.ShapeDtypeStruct(a, BF16))
    t = max(len(turns), 1)
    held = max(sum(k.read < len(far) and (k.turn is not None or k.rows) for k in tasks), 1)
    loads = max(sum(k.read < len(far) for k in tasks), 1)
    m = max(sum(k.turn is not None and k.rows for k in tasks), 1)
    p = max(sum(k.pages for k in tasks), 1)
    f32 = jnp.float32
    return pl.pallas_call(
        functools.partial(step_kernel, len(far), len(near), len(out), len(aliases), tasks, turns),
        out_shape=out,
        in_specs=in_specs,
        out_specs=out_specs,
        input_output_aliases=aliases,
        scratch_shapes=[
            pltpu.VMEM((held, n, size), BF16),
            pltpu.VMEM((m, n, size), BF16),
            pltpu.VMEM((p, n // PAGE, size), BF16),
            pltpu.VMEM((p, n // PAGE, size), BF16),
            pltpu.VMEM((t, size // 2, n), f32),
            pltpu.VMEM((t, n, size), f32),
            pltpu.VMEM((t, n, size), f32),
            pltpu.SemaphoreType.DMA((loads,)),
            pltpu.SemaphoreType.DMA((len(tasks),)),
            pltpu.SemaphoreType.DMA((2, p)),
            pltpu.SemaphoreType.DMA((t,)),
        ],
        cost_estimate=pl.CostEstimate(
            flops=COST * len(tasks), bytes_accessed=4 * len(tasks) * n * size, transcendentals=0
        ),
        compiler_params=pltpu.CompilerParams(vmem_limit_bytes=VMEM_LIMIT),
    )(*operands)


def on_device(fresh_keys, fresh_values, turn_angle):
    keys, values, angles = fresh_keys[:, :, 0], fresh_values[:, :, 0], turn_angle.T
    seqs, n, size = keys.shape
    grown = [(seqs * n, size)] * 2 + [(seqs * n // PAGE, size)] * 2
    near = (1, 3)

    def key_block(e, j):
        return lambda y, z: slot(y + e, z + j)

    def value_block(e, j):
        return lambda y, z: slot(y + j, z + e)

    def from_y(e, j):
        return lambda y, z: slot(y - e, z - j)

    def hop(sent, first, js):
        half = len(sent) // 2
        moved = [shift(a, e if first else 0, 0 if first else e) for a, e in zip(sent[:half], js)]
        return moved, [shift(a, 0 if first else e, e if first else 0) for a, e in zip(sent[half:], js)]

    def pick(es, js):
        tasks = []
        for i, e in enumerate(es):
            tasks += [Task(0, key_block(e, j), i, q) for q, j in enumerate(js)]
        for i, e in enumerate(es):
            tasks += [Task(1, value_block(e, j), len(es) + i, q) for q, j in enumerate(js)]
        sent = step((keys, values), (), None, [len(js)] * (2 * len(es)), [], tasks)
        return hop(sent, True, es)

    k_first, v_first = pick(near, (0,))
    k_rest, v_rest = pick(near, (1, 3, 2))
    second = (1, 3, 2)

    tasks = [Task(0, key_block(0, j), q, 0, 0) for q, j in enumerate(second)]
    tasks += [Task(1, value_block(0, j), 3 + q, 0) for q, j in enumerate(second)]
    tasks.append(Task(0, key_block(0, 0), 6, from_y(0, 0), 0, True, True))
    tasks.append(Task(1, value_block(0, 0), 7, from_y(0, 0), rows=True))
    *sent, a, b, c, d = step((keys, values), (), angles, [1] * 6, grown, tasks)
    grown = [a, b, c, d]
    k_own, v_own = hop(sent[:2] + sent[3:5], False, near)
    k_own2, v_own2 = hop(sent[2:3] + sent[5:6], False, (2,))
    k_far, v_far = pick((2,), (0, 1, 3, 2))

    near_in = (*k_first, *v_first, *k_rest, *v_rest)
    tasks = []
    for q in range(3):
        tasks += [Task(4 + i, q, q, i, e) for i, e in enumerate(near)]
        tasks += [Task(6 + i, q, 3 + q, i) for i, e in enumerate(near)]
    tasks += [Task(i, 0, 6, from_y(e, 0), e, True, True) for i, e in enumerate(near)]
    tasks += [Task(2 + i, 0, 7, from_y(0, e), rows=True) for i, e in enumerate(near)]
    *sent, a, b, c, d = step((), near_in, angles, [2] * 6, grown, tasks)
    grown = [a, b, c, d]
    k_near, v_near = hop(sent[:2] + sent[3:5], False, near)
    k_near2, v_near2 = hop(sent[2:3] + sent[5:6], False, (2,))

    tasks = [Task(0, 1 + q, q, 0, 2) for q in range(3)]
    tasks += [Task(1, 1 + q, 3 + q, 0) for q in range(3)]
    tasks.append(Task(0, 0, 6, from_y(2, 0), 2, True, True))
    tasks.append(Task(1, 0, 7, from_y(0, 2), rows=True))
    *sent, a, b, c, d = step((), (*k_far, *v_far), angles, [1] * 6, grown, tasks)
    grown = [a, b, c, d]
    k_last, v_last = hop(sent[:2] + sent[3:5], False, near)
    k_last2, v_last2 = hop(sent[2:3] + sent[5:6], False, (2,))

    def finish(got, grown):
        tasks, reads = [], []
        for k_got, v_got, js, es in got:
            for a, b, j in zip(k_got, v_got, js):
                at = len(reads)
                reads += [a, b]
                tasks += [Task(at, q, 0, from_y(e, j), None, True, True) for q, e in enumerate(es)]
                tasks += [Task(at + 1, q, 1, from_y(j, e), None, True) for q, e in enumerate(es)]
        return step((), reads, None, [], grown, tasks)

    grown = finish([(k_own, v_own, near, (0,)), (k_own2, v_own2, (2,), (0,))], grown)
    grown = finish([(k_near, v_near, near, near), (k_near2, v_near2, (2,), near)], grown)
    grown = finish([(k_last, v_last, near, (2,))], grown)
    grown = finish([(k_last2, v_last2, (2,), (2,))], grown)
    return tuple(x[None, :, None] for x in grown)


def solution(mesh):
    cut = P(None, SEQ, "model", None)
    out = P(SEQ, None, "model", None)

    return jax.shard_map(on_device, mesh=mesh, in_specs=(cut, cut, P()), out_specs=(out,) * 4, check_vma=False)
```

time: 183 us -> 215 us (1.17)
  the two profiles are of different devices: /device:TPU:0 before, /device:TPU:64 now
where the time goes in v2:
time: 215 us
  waiting for transfers between devices  140 us (65%)
  starting transfers between devices  38.6 us (18%)
  Pallas kernels  35.5 us (17%)
    ppermute x28, waiting for transfers between devices, shift(): return lax.ppermute(a, SEQ, pairs)  140 us
    ppermute x28, starting transfers between devices, shift(): return lax.ppermute(a, SEQ, pairs)  38.6 us
    pallas_call x10, Pallas kernels, step(): pl.pallas_call(functools.partial(step_kernel, len(far), len(near), len(ou...  35.5 us
  transfers between devices with their start and end apart: 28, of which 7 were waited for; matrix products, arithmetic and copies ran while one was open for 0% of the time, Pallas kernels for 15%

profile of v2, /device:TPU:64, one launch (start us, length us, event | category | flops | bytes accessed | tf_op | source)
XLA Modules:
  0.0 215.1 jit_solution(2417442765006590370)
XLA Ops:
  0.6 2.6 %shard_map.68 = (bf16[3,1536,128]{2,1,0:T(8,128)(2,1)S(1)}, bf16[3,1536,128]{2,1,0:T(8,128)(2,1)S(1)}, bf16[3,1536,128]{2,1,0:T(8,128)(2,1)S(1)}, bf16[3,1536,128]{2,1,0:T(8,128)(2,1)S(1)}) custom-call(bf16[16,1536,128]{2,1,0:T(8,128)(2,1)} %bitcast.9, bf16[16,1536,128]{2,1,0:T(8,128)(2,1)} %bitcast.13), custom_call_target="tpu_custom_call" | custom-call | flops 600000000 | bytes 9437184 | tf_op jit(solution)/shard_map/pallas_call | solution.py:194
  7.9 1.7 collective-permute-start.3
  11.6 29.0 %collective-permute-done.2.refs_0_ = bf16[1,1536,128]{2,1,0:T(8,128)(2,1)S(1)} collective-permute-done((bf16[1,1536,128]{2,1,0:T(8,128)(2,1)S(1)}, bf16[1,1536,128]{2,1,0:T(8,128)(2,1)S(1)}, u32[]{:S(2)}, u32[]{:S(2)}) %collective-permute-start.2) | collective-permute-done | bytes 393248 | tf_op jit(solution)/shard_map/ppermute | solution.py:32
  40.7 1.7 collective-permute-start.7
  44.5 6.7 %shard_map.69 = (bf16[1,1536,128]{2,1,0:T(8,128)(2,1)S(1)}, bf16[1,1536,128]{2,1,0:T(8,128)(2,1)S(1)}, bf16[1,1536,128]{2,1,0:T(8,128)(2,1)S(1)}, bf16[1,1536,12...) custom-call(bf16[16,1536,128]{2,1,0:T(8,128)(2,1)} %bitcast.11, ...), custom_call_target="tpu_custom_call" | custom-call | flops 400000000 | bytes 6291456 | tf_op jit(solution)/shard_map/pallas_call | solution.py:194
  51.2 1.7 collective-permute-start.22
  52.9 2.0 shard_map.66
  54.9 22.5 %collective-permute-done.22.refs_0_ = bf16[1,1536,128]{2,1,0:T(8,128)(2,1)S(1)} collective-permute-done((bf16[1,1536,128]{2,1,0:T(8,128)(2,1)S(1)}, bf16[1,1536,128]{2,1,0:T(8,128)(2,1)S(1)}, u32[]{:S(2)}, u32[]{:S(2)}) %collective-permute-start.22) | collective-permute-done | bytes 393248 | tf_op jit(solution)/shard_map/ppermute | solution.py:32
  78.1 1.9 collective-permute-start.1
  82.1 2.3 %collective-permute-start.25 = (bf16[1,1536,128]{2,1,0:T(8,128)(2,1)S(1)}, bf16[1,1536,128]{2,1,0:T(8,128)(2,1)S(1)}, u32[]{:S(2)}, u32[]{:S(2)}) collective-permute-start(bf16[1,1536,128]{2,1,0:T(8,128)(2,1)S(1)} %get-tuple-element.93), channel_id=1, source_target_pairs={{0,24},{8,0},{16,8},{24,16},{32,56},{40,32},{48,40},{56,48},{64,88... | collective-permute-start | bytes 1179656 | tf_op jit(solution)/shard_map/ppermute | solution.py:32
  84.4 10.4 %shard_map.70 = (bf16[2,1536,128]{2,1,0:T(8,128)(2,1)S(1)}, bf16[2,1536,128]{2,1,0:T(8,128)(2,1)S(1)}, bf16[2,1536,128]{2,1,0:T(8,128)(2,1)S(1)}, bf16[2,1536,12...) custom-call(bf16[1,1536,128]{2,1,0:T(8,128)(2,1)S(1)} %collective-pe, ...), custom_call_target="tpu_custom_call", output_to_operand_aliasing={{6}: (9, {}), {7}: (10, {}), {8}: (11, {}), {9}: (12, {})} | custom-call | flops 800000000 | bytes 12582912 | tf_op jit(solution)/shard_map/pallas_call | solution.py:194
  94.8 26.7 %collective-permute-done.23.refs_1_ = bf16[1,1536,128]{2,1,0:T(8,128)(2,1)S(1)} collective-permute-done((bf16[1,1536,128]{2,1,0:T(8,128)(2,1)S(1)}, bf16[1,1536,128]{2,1,0:T(8,128)(2,1)S(1)}, u32[]{:S(2)}, u32[]{:S(2)}) %collective-permute-start.23) | collective-permute-done | bytes 393248 | tf_op jit(solution)/shard_map/ppermute | solution.py:32
  123.7 2.1 collective-permute-start.27
  125.8 24.1 %collective-permute-done.26.refs_4_ = bf16[1,1536,128]{2,1,0:T(8,128)(2,1)S(1)} collective-permute-done((bf16[1,1536,128]{2,1,0:T(8,128)(2,1)S(1)}, bf16[1,1536,128]{2,1,0:T(8,128)(2,1)S(1)}, u32[]{:S(2)}, u32[]{:S(2)}) %collective-permute-start.26) | collective-permute-done | bytes 393248 | tf_op jit(solution)/shard_map/ppermute | solution.py:32
  149.9 3.3 %collective-permute-start.19 = (bf16[2,1536,128]{2,1,0:T(8,128)(2,1)S(1)}, bf16[2,1536,128]{2,1,0:T(8,128)(2,1)S(1)}, u32[]{:S(2)}, u32[]{:S(2)}) collective-permute-start(bf16[2,1536,128]{2,1,0:T(8,128)(2,1)S(1)} %get-tuple-element.87), channel_id=1, source_target_pairs={{0,24},{8,0},{16,8},{24,16},{32,56},{40,32},{48,40},{56,48},{64,88... | collective-permute-start | bytes 2359304 | tf_op jit(solution)/shard_map/ppermute | solution.py:32
  153.2 2.7 %collective-permute-start.20 = (bf16[2,1536,128]{2,1,0:T(8,128)(2,1)S(1)}, bf16[2,1536,128]{2,1,0:T(8,128)(2,1)S(1)}, u32[]{:S(2)}, u32[]{:S(2)}) collective-permute-start(bf16[2,1536,128]{2,1,0:T(8,128)(2,1)S(1)} %get-tuple-element.88), channel_id=1, source_target_pairs={{0,64},{8,72},{16,80},{24,88},{32,96},{40,104},{48,112},{56,120},{... | collective-permute-start | bytes 2359304 | tf_op jit(solution)/shard_map/ppermute | solution.py:32
  155.9 6.0 %shard_map.71 = (bf16[1,1536,128]{2,1,0:T(8,128)(2,1)S(1)}, bf16[1,1536,128]{2,1,0:T(8,128)(2,1)S(1)}, bf16[1,1536,128]{2,1,0:T(8,128)(2,1)S(1)}, bf16[1,1536,12...) custom-call(bf16[4,1536,128]{2,1,0:T(8,128)(2,1)S(1)} %collective-pe, ...), custom_call_target="tpu_custom_call", output_to_operand_aliasing={{6}: (3, {}), {7}: (4, {}), {8}: (5, {}), {9}: (6, {})} | custom-call | flops 400000000 | bytes 6291456 | tf_op jit(solution)/shard_map/pallas_call | solution.py:194
  161.9 24.9 %collective-permute-done.17.refs_1_ = bf16[2,1536,128]{2,1,0:T(8,128)(2,1)S(1)} collective-permute-done((bf16[2,1536,128]{2,1,0:T(8,128)(2,1)S(1)}, bf16[2,1536,128]{2,1,0:T(8,128)(2,1)S(1)}, u32[]{:S(2)}, u32[]{:S(2)}) %collective-permute-start.17) | collective-permute-done | bytes 786464 | tf_op jit(solution)/shard_map/ppermute | solution.py:32
  186.9 2.1 collective-permute-start.14
  188.9 3.6 %collective-permute-start.15 = (bf16[1,1536,128]{2,1,0:T(8,128)(2,1)S(1)}, bf16[1,1536,128]{2,1,0:T(8,128)(2,1)S(1)}, u32[]{:S(2)}, u32[]{:S(2)}) collective-permute-start(bf16[1,1536,128]{2,1,0:T(8,128)(2,1)S(1)} %get-tuple-element.83), channel_id=1, source_target_pairs={{0,24},{8,0},{16,8},{24,16},{32,56},{40,32},{48,40},{56,48},{64,88... | collective-permute-start | bytes 1179656 | tf_op jit(solution)/shard_map/ppermute | solution.py:32
  192.5 3.2 %collective-permute-start.10 = (bf16[1,1536,128]{2,1,0:T(8,128)(2,1)S(1)}, bf16[1,1536,128]{2,1,0:T(8,128)(2,1)S(1)}, u32[]{:S(2)}, u32[]{:S(2)}) collective-permute-start(bf16[1,1536,128]{2,1,0:T(8,128)(2,1)S(1)} %get-tuple-element.78), channel_id=1, source_target_pairs={{0,64},{8,72},{16,80},{24,88},{32,96},{40,104},{48,112},{56,120},{... | collective-permute-start | bytes 1179656 | tf_op jit(solution)/shard_map/ppermute | solution.py:32
  195.7 9.1 %collective-permute-done.12.refs_0_ = bf16[1,1536,128]{2,1,0:T(8,128)(2,1)S(1)} collective-permute-done((bf16[1,1536,128]{2,1,0:T(8,128)(2,1)S(1)}, bf16[1,1536,128]{2,1,0:T(8,128)(2,1)S(1)}, u32[]{:S(2)}, u32[]{:S(2)}) %collective-permute-start.12) | collective-permute-done | bytes 393248 | tf_op jit(solution)/shard_map/ppermute | solution.py:32
  206.5 2.6 %shard_map.73 = (bf16[24576,128]{1,0:T(8,128)(2,1)}, bf16[24576,128]{1,0:T(8,128)(2,1)}, bf16[768,128]{1,0:T(8,128)(2,1)}, bf16[768,128]{1,0:T(8,128)(2,1)}) custom-call(bf16[2,1536,128]{2,1,0:T(8,128)(2,1)S(1)} %collective-permute-done.16.refs_0_, ...), custom_call_target="tpu_custom_call", output_to_operand_aliasing={{0}: (6, {}), {1}: (7, {}), {2}: (8, {}), {3}: (9, {})} | custom-call | flops 600000000 | bytes 9437184 | tf_op jit(solution)/shard_map/pallas_call | solution.py:194
  210.4 3.7 %collective-permute-done.11.refs_1_ = bf16[1,1536,128]{2,1,0:T(8,128)(2,1)S(1)} collective-permute-done((bf16[1,1536,128]{2,1,0:T(8,128)(2,1)S(1)}, bf16[1,1536,128]{2,1,0:T(8,128)(2,1)S(1)}, u32[]{:S(2)}, u32[]{:S(2)}) %collective-permute-start.11) | collective-permute-done | bytes 393248 | tf_op jit(solution)/shard_map/ppermute | solution.py:32
  (42 shorter events, 17.7 us)
Async XLA Ops:
  3.2 74.9 %collective-permute-start.6 = (bf16[3,1536,128]{2,1,0:T(8,128)(2,1)S(1)}, bf16[3,1536,128]{2,1,0:T(8,128)(2,1)S(1)}, u32[]{:S(2)}, u32[]{:S(2)}) collective-permute-start(bf16[3,1536,128]{2,1,0:T(8,128)(2,1)S(1)} %get-tuple-element.66), channel_id=1, source_target_pairs={{0,8},{8,16},{16,24},{24,0},{32,40},{40,48},{48,56},{56,32},{64,72... | collective-permute-start | bytes 3538952 | tf_op jit(solution)/shard_map/ppermute | solution.py:32
  6.3 34.4 %collective-permute-start.2 = (bf16[1,1536,128]{2,1,0:T(8,128)(2,1)S(1)}, bf16[1,1536,128]{2,1,0:T(8,128)(2,1)S(1)}, u32[]{:S(2)}, u32[]{:S(2)}) collective-permute-start(bf16[1,1536,128]{2,1,0:T(8,128)(2,1)S(1)} %get-tuple-element.62), channel_id=1, source_target_pairs={{0,8},{8,16},{16,24},{24,0},{32,40},{40,48},{48,56},{56,32},{64,72... | collective-permute-start | bytes 1179656 | tf_op jit(solution)/shard_map/ppermute | solution.py:32
  7.9 34.5 %collective-permute-start.3 = (bf16[1,1536,128]{2,1,0:T(8,128)(2,1)S(1)}, bf16[1,1536,128]{2,1,0:T(8,128)(2,1)S(1)}, u32[]{:S(2)}, u32[]{:S(2)}) collective-permute-start(bf16[1,1536,128]{2,1,0:T(8,128)(2,1)S(1)} %get-tuple-element.63), channel_id=1, source_target_pairs={{0,24},{8,0},{16,8},{24,16},{32,56},{40,32},{48,40},{56,48},{64,88... | collective-permute-start | bytes 1179656 | tf_op jit(solution)/shard_map/ppermute | solution.py:32
  9.6 34.4 %collective-permute-start.4 = (bf16[1,1536,128]{2,1,0:T(8,128)(2,1)S(1)}, bf16[1,1536,128]{2,1,0:T(8,128)(2,1)S(1)}, u32[]{:S(2)}, u32[]{:S(2)}) collective-permute-start(bf16[1,1536,128]{2,1,0:T(8,128)(2,1)S(1)} %get-tuple-element.64), channel_id=1, source_target_pairs={{0,32},{8,40},{16,48},{24,56},{32,64},{40,72},{48,80},{56,88},{64,... | collective-permute-start | bytes 1179656 | tf_op jit(solution)/shard_map/ppermute | solution.py:32
  11.2 40.0 %collective-permute-start.5 = (bf16[1,1536,128]{2,1,0:T(8,128)(2,1)S(1)}, bf16[1,1536,128]{2,1,0:T(8,128)(2,1)S(1)}, u32[]{:S(2)}, u32[]{:S(2)}) collective-permute-start(bf16[1,1536,128]{2,1,0:T(8,128)(2,1)S(1)} %get-tuple-element.65), channel_id=1, source_target_pairs={{0,96},{8,104},{16,112},{24,120},{32,0},{40,8},{48,16},{56,24},{64... | collective-permute-start | bytes 1179656 | tf_op jit(solution)/shard_map/ppermute | solution.py:32
  40.7 39.3 %collective-permute-start.7 = (bf16[3,1536,128]{2,1,0:T(8,128)(2,1)S(1)}, bf16[3,1536,128]{2,1,0:T(8,128)(2,1)S(1)}, u32[]{:S(2)}, u32[]{:S(2)}) collective-permute-start(bf16[3,1536,128]{2,1,0:T(8,128)(2,1)S(1)} %get-tuple-element.67), channel_id=1, source_target_pairs={{0,24},{8,0},{16,8},{24,16},{32,56},{40,32},{48,40},{56,48},{64,88... | collective-permute-start | bytes 3538952 | tf_op jit(solution)/shard_map/ppermute | solution.py:32
  42.4 38.6 %collective-permute-start.8 = (bf16[3,1536,128]{2,1,0:T(8,128)(2,1)S(1)}, bf16[3,1536,128]{2,1,0:T(8,128)(2,1)S(1)}, u32[]{:S(2)}, u32[]{:S(2)}) collective-permute-start(bf16[3,1536,128]{2,1,0:T(8,128)(2,1)S(1)} %get-tuple-element.68), channel_id=1, source_target_pairs={{0,32},{8,40},{16,48},{24,56},{32,64},{40,72},{48,80},{56,88},{64,... | collective-permute-start | bytes 3538952 | tf_op jit(solution)/shard_map/ppermute | solution.py:32
  44.1 38.1 %collective-permute-start.9 = (bf16[3,1536,128]{2,1,0:T(8,128)(2,1)S(1)}, bf16[3,1536,128]{2,1,0:T(8,128)(2,1)S(1)}, u32[]{:S(2)}, u32[]{:S(2)}) collective-permute-start(bf16[3,1536,128]{2,1,0:T(8,128)(2,1)S(1)} %get-tuple-element.69), channel_id=1, source_target_pairs={{0,96},{8,104},{16,112},{24,120},{32,0},{40,8},{48,16},{56,24},{64... | collective-permute-start | bytes 3538952 | tf_op jit(solution)/shard_map/ppermute | solution.py:32
  51.2 26.2 %collective-permute-start.22 = (bf16[1,1536,128]{2,1,0:T(8,128)(2,1)S(1)}, bf16[1,1536,128]{2,1,0:T(8,128)(2,1)S(1)}, u32[]{:S(2)}, u32[]{:S(2)}) collective-permute-start(bf16[1,1536,128]{2,1,0:T(8,128)(2,1)S(1)} %get-tuple-element.90), channel_id=1, source_target_pairs={{0,32},{8,40},{16,48},{24,56},{32,64},{40,72},{48,80},{56,88},{64,... | collective-permute-start | bytes 1179656 | tf_op jit(solution)/shard_map/ppermute | solution.py:32
  77.4 72.5 %collective-permute-start = (bf16[4,1536,128]{2,1,0:T(8,128)(2,1)S(1)}, bf16[4,1536,128]{2,1,0:T(8,128)(2,1)S(1)}, u32[]{:S(2)}, u32[]{:S(2)}) collective-permute-start(bf16[4,1536,128]{2,1,0:T(8,128)(2,1)S(1)} %get-tuple-element.60), channel_id=1, source_target_pairs={{0,16},{8,24},{16,0},{24,8},{32,48},{40,56},{48,32},{56,40},{64,80... | collective-permute-start | bytes 4718600 | tf_op jit(solution)/shard_map/ppermute | solution.py:32
  78.1 75.1 %collective-permute-start.1 = (bf16[4,1536,128]{2,1,0:T(8,128)(2,1)S(1)}, bf16[4,1536,128]{2,1,0:T(8,128)(2,1)S(1)}, u32[]{:S(2)}, u32[]{:S(2)}) collective-permute-start(bf16[4,1536,128]{2,1,0:T(8,128)(2,1)S(1)} %get-tuple-element.61), channel_id=1, source_target_pairs={{0,64},{8,72},{16,80},{24,88},{32,96},{40,104},{48,112},{56,120},{... | collective-permute-start | bytes 4718600 | tf_op jit(solution)/shard_map/ppermute | solution.py:32
  80.0 41.5 %collective-permute-start.23 = (bf16[1,1536,128]{2,1,0:T(8,128)(2,1)S(1)}, bf16[1,1536,128]{2,1,0:T(8,128)(2,1)S(1)}, u32[]{:S(2)}, u32[]{:S(2)}) collective-permute-start(bf16[1,1536,128]{2,1,0:T(8,128)(2,1)S(1)} %get-tuple-element.91), channel_id=1, source_target_pairs={{0,8},{8,16},{16,24},{24,0},{32,40},{40,48},{48,56},{56,32},{64,72... | collective-permute-start | bytes 1179656 | tf_op jit(solution)/shard_map/ppermute | solution.py:32
  81.0 42.1 %collective-permute-start.24 = (bf16[1,1536,128]{2,1,0:T(8,128)(2,1)S(1)}, bf16[1,1536,128]{2,1,0:T(8,128)(2,1)S(1)}, u32[]{:S(2)}, u32[]{:S(2)}) collective-permute-start(bf16[1,1536,128]{2,1,0:T(8,128)(2,1)S(1)} %get-tuple-element.92), channel_id=1, source_target_pairs={{0,96},{8,104},{16,112},{24,120},{32,0},{40,8},{48,16},{56,24},{64... | collective-permute-start | bytes 1179656 | tf_op jit(solution)/shard_map/ppermute | solution.py:32
  82.1 41.6 %collective-permute-start.25 = (bf16[1,1536,128]{2,1,0:T(8,128)(2,1)S(1)}, bf16[1,1536,128]{2,1,0:T(8,128)(2,1)S(1)}, u32[]{:S(2)}, u32[]{:S(2)}) collective-permute-start(bf16[1,1536,128]{2,1,0:T(8,128)(2,1)S(1)} %get-tuple-element.93), channel_id=1, source_target_pairs={{0,24},{8,0},{16,8},{24,16},{32,56},{40,32},{48,40},{56,48},{64,88... | collective-permute-start | bytes 1179656 | tf_op jit(solution)/shard_map/ppermute | solution.py:32
  121.5 34.4 %collective-permute-start.16 = (bf16[2,1536,128]{2,1,0:T(8,128)(2,1)S(1)}, bf16[2,1536,128]{2,1,0:T(8,128)(2,1)S(1)}, u32[]{:S(2)}, u32[]{:S(2)}) collective-permute-start(bf16[2,1536,128]{2,1,0:T(8,128)(2,1)S(1)} %get-tuple-element.84), channel_id=1, source_target_pairs={{0,32},{8,40},{16,48},{24,56},{32,64},{40,72},{48,80},{56,88},{64,... | collective-permute-start | bytes 2359304 | tf_op jit(solution)/shard_map/ppermute | solution.py:32
  123.1 26.7 %collective-permute-start.26 = (bf16[1,1536,128]{2,1,0:T(8,128)(2,1)S(1)}, bf16[1,1536,128]{2,1,0:T(8,128)(2,1)S(1)}, u32[]{:S(2)}, u32[]{:S(2)}) collective-permute-start(bf16[1,1536,128]{2,1,0:T(8,128)(2,1)S(1)} %get-tuple-element.94), channel_id=1, source_target_pairs={{0,64},{8,72},{16,80},{24,88},{32,96},{40,104},{48,112},{56,120},{... | collective-permute-start | bytes 1179656 | tf_op jit(solution)/shard_map/ppermute | solution.py:32
  123.7 26.1 %collective-permute-start.27 = (bf16[1,1536,128]{2,1,0:T(8,128)(2,1)S(1)}, bf16[1,1536,128]{2,1,0:T(8,128)(2,1)S(1)}, u32[]{:S(2)}, u32[]{:S(2)}) collective-permute-start(bf16[1,1536,128]{2,1,0:T(8,128)(2,1)S(1)} %get-tuple-element.95), channel_id=1, source_target_pairs={{0,16},{8,24},{16,0},{24,8},{32,48},{40,56},{48,32},{56,40},{64,80... | collective-permute-start | bytes 1179656 | tf_op jit(solution)/shard_map/ppermute | solution.py:32
  149.9 37.0 %collective-permute-start.17 = (bf16[2,1536,128]{2,1,0:T(8,128)(2,1)S(1)}, bf16[2,1536,128]{2,1,0:T(8,128)(2,1)S(1)}, u32[]{:S(2)}, u32[]{:S(2)}) collective-permute-start(bf16[2,1536,128]{2,1,0:T(8,128)(2,1)S(1)} %get-tuple-element.85), channel_id=1, source_target_pairs={{0,8},{8,16},{16,24},{24,0},{32,40},{40,48},{48,56},{56,32},{64,72... | collective-permute-start | bytes 2359304 | tf_op jit(solution)/shard_map/ppermute | solution.py:32
  149.9 37.0 %collective-permute-start.18 = (bf16[2,1536,128]{2,1,0:T(8,128)(2,1)S(1)}, bf16[2,1536,128]{2,1,0:T(8,128)(2,1)S(1)}, u32[]{:S(2)}, u32[]{:S(2)}) collective-permute-start(bf16[2,1536,128]{2,1,0:T(8,128)(2,1)S(1)} %get-tuple-element.86), channel_id=1, source_target_pairs={{0,96},{8,104},{16,112},{24,120},{32,0},{40,8},{48,16},{56,24},{64... | collective-permute-start | bytes 2359304 | tf_op jit(solution)/shard_map/ppermute | solution.py:32
  149.9 36.9 %collective-permute-start.19 = (bf16[2,1536,128]{2,1,0:T(8,128)(2,1)S(1)}, bf16[2,1536,128]{2,1,0:T(8,128)(2,1)S(1)}, u32[]{:S(2)}, u32[]{:S(2)}) collective-permute-start(bf16[2,1536,128]{2,1,0:T(8,128)(2,1)S(1)} %get-tuple-element.87), channel_id=1, source_target_pairs={{0,24},{8,0},{16,8},{24,16},{32,56},{40,32},{48,40},{56,48},{64,88... | collective-permute-start | bytes 2359304 | tf_op jit(solution)/shard_map/ppermute | solution.py:32
  153.2 35.7 %collective-permute-start.20 = (bf16[2,1536,128]{2,1,0:T(8,128)(2,1)S(1)}, bf16[2,1536,128]{2,1,0:T(8,128)(2,1)S(1)}, u32[]{:S(2)}, u32[]{:S(2)}) collective-permute-start(bf16[2,1536,128]{2,1,0:T(8,128)(2,1)S(1)} %get-tuple-element.88), channel_id=1, source_target_pairs={{0,64},{8,72},{16,80},{24,88},{32,96},{40,104},{48,112},{56,120},{... | collective-permute-start | bytes 2359304 | tf_op jit(solution)/shard_map/ppermute | solution.py:32
  155.9 36.5 %collective-permute-start.21 = (bf16[2,1536,128]{2,1,0:T(8,128)(2,1)S(1)}, bf16[2,1536,128]{2,1,0:T(8,128)(2,1)S(1)}, u32[]{:S(2)}, u32[]{:S(2)}) collective-permute-start(bf16[2,1536,128]{2,1,0:T(8,128)(2,1)S(1)} %get-tuple-element.89), channel_id=1, source_target_pairs={{0,16},{8,24},{16,0},{24,8},{32,48},{40,56},{48,32},{56,40},{64,80... | collective-permute-start | bytes 2359304 | tf_op jit(solution)/shard_map/ppermute | solution.py:32
  186.8 22.2 %collective-permute-start.13 = (bf16[1,1536,128]{2,1,0:T(8,128)(2,1)S(1)}, bf16[1,1536,128]{2,1,0:T(8,128)(2,1)S(1)}, u32[]{:S(2)}, u32[]{:S(2)}) collective-permute-start(bf16[1,1536,128]{2,1,0:T(8,128)(2,1)S(1)} %get-tuple-element.81), channel_id=1, source_target_pairs={{0,8},{8,16},{16,24},{24,0},{32,40},{40,48},{48,56},{56,32},{64,72... | collective-permute-start | bytes 1179656 | tf_op jit(solution)/shard_map/ppermute | solution.py:32
  186.9 22.2 %collective-permute-start.14 = (bf16[1,1536,128]{2,1,0:T(8,128)(2,1)S(1)}, bf16[1,1536,128]{2,1,0:T(8,128)(2,1)S(1)}, u32[]{:S(2)}, u32[]{:S(2)}) collective-permute-start(bf16[1,1536,128]{2,1,0:T(8,128)(2,1)S(1)} %get-tuple-element.82), channel_id=1, source_target_pairs={{0,96},{8,104},{16,112},{24,120},{32,0},{40,8},{48,16},{56,24},{64... | collective-permute-start | bytes 1179656 | tf_op jit(solution)/shard_map/ppermute | solution.py:32
  (4 other events, 65.3 us)

commit v3 on v2

--- a/solution.py
+++ b/solution.py
@@ -140,27 +140,30 @@
             lax.fori_loop(0, n // 256, copy, 0)
         if not task.rows:
             continue
+        ready[k] = block
         index = value_at(task.index, y, z)
         to = outs[task.to].at[pl.ds(pl.multiple_of(index * n, n), n)]
         stores.append(pltpu.make_async_copy(block, to, out_sem.at[k]))
         stores[-1].start()
-        if task.pages:
-            count, group = n // PAGE, 16
-
-            def bound(q, _, block=block, p=p):
-                rows = block[pl.ds(pl.multiple_of(q * group * PAGE, group * PAGE), group * PAGE), :]
-                rows = rows.reshape(group, PAGE, size)
-                r = pl.ds(pl.multiple_of(q * group, group), group)
-                high[p, r, :] = jnp.max(rows, axis=1)
-                low[p, r, :] = jnp.min(rows, axis=1)
-                return 0
-
-            lax.fori_loop(0, count // group, bound, 0)
-            for i, side in enumerate((high, low)):
-                to = outs[writes - 2 + i].at[pl.ds(pl.multiple_of(index * count, 16), count)]
-                stores.append(pltpu.make_async_copy(side.at[p], to, page_sem.at[i, p]))
-                stores[-1].start()
-            p += 1
+    count, group = n // PAGE, 16
+    for k, task in enumerate(tasks):
+        if not task.pages:
+            continue
+
+        def bound(q, _, block=ready[k], p=p):
+            rows = block[pl.ds(pl.multiple_of(q * group * PAGE, group * PAGE), group * PAGE), :]
+            rows = rows.reshape(group, PAGE, size)
+            r = pl.ds(pl.multiple_of(q * group, group), group)
+            high[p, r, :] = jnp.max(rows, axis=1)
+            low[p, r, :] = jnp.min(rows, axis=1)
+            return 0
+
+        lax.fori_loop(0, count // group, bound, 0, unroll=True)
+        for i, side in enumerate((high, low)):
+            to = outs[writes - 2 + i].at[pl.ds(pl.multiple_of(value_at(task.index, y, z) * count, 16), count)]
+            stores.append(pltpu.make_async_copy(side.at[p], to, page_sem.at[i, p]))
+            stores[-1].start()
+        p += 1
     for store in stores:
         store.wait()
 
@@ -246,8 +249,8 @@
         sent = step((keys, values), (), None, [len(js)] * (2 * len(es)), [], tasks)
         return hop(sent, True, es)
 
-    k_first, v_first = pick(near, (0,))
-    k_rest, v_rest = pick(near, (1, 3, 2))
+    k_first, v_first = pick((2,), (0, 1))
+    k_rest, v_rest = pick(near, (0, 1, 3, 2))
     second = (1, 3, 2)
 
     tasks = [Task(0, key_block(0, j), q, 0, 0) for q, j in enumerate(second)]
@@ -258,13 +261,13 @@
     grown = [a, b, c, d]
     k_own, v_own = hop(sent[:2] + sent[3:5], False, near)
     k_own2, v_own2 = hop(sent[2:3] + sent[5:6], False, (2,))
-    k_far, v_far = pick((2,), (0, 1, 3, 2))
-
-    near_in = (*k_first, *v_first, *k_rest, *v_rest)
+    k_far, v_far = pick((2,), (3, 2))
+
+    near_in = (*k_rest, *v_rest)
     tasks = []
     for q in range(3):
-        tasks += [Task(4 + i, q, q, i, e) for i, e in enumerate(near)]
-        tasks += [Task(6 + i, q, 3 + q, i) for i, e in enumerate(near)]
+        tasks += [Task(i, 1 + q, q, i, e) for i, e in enumerate(near)]
+        tasks += [Task(2 + i, 1 + q, 3 + q, i) for i, e in enumerate(near)]
     tasks += [Task(i, 0, 6, from_y(e, 0), e, True, True) for i, e in enumerate(near)]
     tasks += [Task(2 + i, 0, 7, from_y(0, e), rows=True) for i, e in enumerate(near)]
     *sent, a, b, c, d = step((), near_in, angles, [2] * 6, grown, tasks)
@@ -272,11 +275,13 @@
     k_near, v_near = hop(sent[:2] + sent[3:5], False, near)
     k_near2, v_near2 = hop(sent[2:3] + sent[5:6], False, (2,))
 
-    tasks = [Task(0, 1 + q, q, 0, 2) for q in range(3)]
-    tasks += [Task(1, 1 + q, 3 + q, 0) for q in range(3)]
+    parts = ((0, 1), (2, 0), (2, 1))
+    tasks = [Task(i, at, q, 0, 2) for q, (i, at) in enumerate(parts)]
+    tasks += [Task(i + 1, at, 3 + q, 0) for q, (i, at) in enumerate(parts)]
     tasks.append(Task(0, 0, 6, from_y(2, 0), 2, True, True))
     tasks.append(Task(1, 0, 7, from_y(0, 2), rows=True))
-    *sent, a, b, c, d = step((), (*k_far, *v_far), angles, [1] * 6, grown, tasks)
+    far_in = (*k_first, *v_first, *k_far, *v_far)
+    *sent, a, b, c, d = step((), far_in, angles, [1] * 6, grown, tasks)
     grown = [a, b, c, d]
     k_last, v_last = hop(sent[:2] + sent[3:5], False, near)
     k_last2, v_last2 = hop(sent[2:3] + sent[5:6], False, (2,))

time: 215 us -> 180 us (0.84)
  the two profiles are of different devices: /device:TPU:64 before, /device:TPU:0 now
where the time goes in v3:
time: 180 us; the launch traced here: 179 us
  waiting for transfers between devices  107 us (59%)
  starting transfers between devices  36.1 us (20%)
  Pallas kernels  35.1 us (20%)
    ppermute x26, waiting for transfers between devices, shift(): return lax.ppermute(a, SEQ, pairs)  107 us
    ppermute x26, starting transfers between devices, shift(): return lax.ppermute(a, SEQ, pairs)  36.1 us
    pallas_call x10, Pallas kernels, step(): pl.pallas_call(functools.partial(step_kernel, len(far), len(near), len(ou...  35.1 us
  transfers between devices with their start and end apart: 26, of which 11 were waited for; matrix products, arithmetic and copies ran while one was open for 0% of the time, Pallas kernels for 17%

profile of v3, /device:TPU:0, one launch (start us, length us, event | category | flops | bytes accessed | tf_op | source)
XLA Modules:
  0.0 179.2 jit_solution(13051335163962524241)
XLA Ops:
  0.6 3.1 %shard_map.68 = (bf16[4,1536,128]{2,1,0:T(8,128)(2,1)S(1)}, bf16[4,1536,128]{2,1,0:T(8,128)(2,1)S(1)}, bf16[4,1536,128]{2,1,0:T(8,128)(2,1)S(1)}, bf16[4,1536,128]{2,1,0:T(8,128)(2,1)S(1)}) custom-call(bf16[16,1536,128]{2,1,0:T(8,128)(2,1)} %bitcast.9, bf16[16,1536,128]{2,1,0:T(8,128)(2,1)} %bitcast.13), custom_call_target="tpu_custom_call" | custom-call | flops 800000000 | bytes 12582912 | tf_op jit(solution)/shard_map/pallas_call | solution.py:197
  7.1 2.0 %collective-permute-start.6 = (bf16[4,1536,128]{2,1,0:T(8,128)(2,1)S(1)}, bf16[4,1536,128]{2,1,0:T(8,128)(2,1)S(1)}, u32[]{:S(2)}, u32[]{:S(2)}) collective-permute-start(bf16[4,1536,128]{2,1,0:T(8,128)(2,1)S(1)} %get-tuple-element.64), channel_id=1, source_target_pairs={{0,32},{8,40},{16,48},{24,56},{32,64},{40,72},{48,80},{56,88},{64,... | collective-permute-start | bytes 4718600 | tf_op jit(solution)/shard_map/ppermute | solution.py:32
  9.1 2.1 %collective-permute-start.7 = (bf16[4,1536,128]{2,1,0:T(8,128)(2,1)S(1)}, bf16[4,1536,128]{2,1,0:T(8,128)(2,1)S(1)}, u32[]{:S(2)}, u32[]{:S(2)}) collective-permute-start(bf16[4,1536,128]{2,1,0:T(8,128)(2,1)S(1)} %get-tuple-element.65), channel_id=1, source_target_pairs={{0,96},{8,104},{16,112},{24,120},{32,0},{40,8},{48,16},{56,24},{64... | collective-permute-start | bytes 4718600 | tf_op jit(solution)/shard_map/ppermute | solution.py:32
  11.2 6.7 %shard_map.69 = (bf16[1,1536,128]{2,1,0:T(8,128)(2,1)S(1)}, bf16[1,1536,128]{2,1,0:T(8,128)(2,1)S(1)}, bf16[1,1536,128]{2,1,0:T(8,128)(2,1)S(1)}, bf16[1,1536,12...) custom-call(bf16[16,1536,128]{2,1,0:T(8,128)(2,1)} %bitcast.10, ...), custom_call_target="tpu_custom_call" | custom-call | flops 400000000 | bytes 6291456 | tf_op jit(solution)/shard_map/pallas_call | solution.py:197
  18.0 35.6 %collective-permute-done.20.refs_0_ = bf16[1,1536,128]{2,1,0:T(8,128)(2,1)S(1)} collective-permute-done((bf16[1,1536,128]{2,1,0:T(8,128)(2,1)S(1)}, bf16[1,1536,128]{2,1,0:T(8,128)(2,1)S(1)}, u32[]{:S(2)}, u32[]{:S(2)}) %collective-permute-start.20) | collective-permute-done | bytes 393248 | tf_op jit(solution)/shard_map/ppermute | solution.py:32
  55.3 9.4 %collective-permute-done.21.refs_1_ = bf16[1,1536,128]{2,1,0:T(8,128)(2,1)S(1)} collective-permute-done((bf16[1,1536,128]{2,1,0:T(8,128)(2,1)S(1)}, bf16[1,1536,128]{2,1,0:T(8,128)(2,1)S(1)}, u32[]{:S(2)}, u32[]{:S(2)}) %collective-permute-start.21) | collective-permute-done | bytes 393248 | tf_op jit(solution)/shard_map/ppermute | solution.py:32
  68.0 3.0 %collective-permute-start.2 = (bf16[2,1536,128]{2,1,0:T(8,128)(2,1)S(1)}, bf16[2,1536,128]{2,1,0:T(8,128)(2,1)S(1)}, u32[]{:S(2)}, u32[]{:S(2)}) collective-permute-start(bf16[2,1536,128]{2,1,0:T(8,128)(2,1)S(1)} %get-tuple-element.60), channel_id=1, source_target_pairs={{0,16},{8,24},{16,0},{24,8},{32,48},{40,56},{48,32},{56,40},{64,80... | collective-permute-start | bytes 2359304 | tf_op jit(solution)/shard_map/ppermute | solution.py:32
  71.1 2.2 %collective-permute-start.3 = (bf16[2,1536,128]{2,1,0:T(8,128)(2,1)S(1)}, bf16[2,1536,128]{2,1,0:T(8,128)(2,1)S(1)}, u32[]{:S(2)}, u32[]{:S(2)}) collective-permute-start(bf16[2,1536,128]{2,1,0:T(8,128)(2,1)S(1)} %get-tuple-element.61), channel_id=1, source_target_pairs={{0,64},{8,72},{16,80},{24,88},{32,96},{40,104},{48,112},{56,120},{... | collective-permute-start | bytes 2359304 | tf_op jit(solution)/shard_map/ppermute | solution.py:32
  74.7 10.3 %shard_map.70 = (bf16[2,1536,128]{2,1,0:T(8,128)(2,1)S(1)}, bf16[2,1536,128]{2,1,0:T(8,128)(2,1)S(1)}, bf16[2,1536,128]{2,1,0:T(8,128)(2,1)S(1)}, bf16[2,1536,12...) custom-call(bf16[4,1536,128]{2,1,0:T(8,128)(2,1)S(1)} %collective-pe, ...), custom_call_target="tpu_custom_call", output_to_operand_aliasing={{6}: (5, {}), {7}: (6, {}), {8}: (7, {}), {9}: (8, {})} | custom-call | flops 800000000 | bytes 12582912 | tf_op jit(solution)/shard_map/pallas_call | solution.py:197
  86.6 2.1 %collective-permute-done.1.refs_1_ = bf16[2,1536,128]{2,1,0:T(8,128)(2,1)S(1)} collective-permute-done((bf16[2,1536,128]{2,1,0:T(8,128)(2,1)S(1)}, bf16[2,1536,128]{2,1,0:T(8,128)(2,1)S(1)}, u32[]{:S(2)}, u32[]{:S(2)}) %collective-permute-start.1) | collective-permute-done | bytes 786464 | tf_op jit(solution)/shard_map/ppermute | solution.py:32
  90.0 10.5 %collective-permute-done.2.refs_2_ = bf16[2,1536,128]{2,1,0:T(8,128)(2,1)S(1)} collective-permute-done((bf16[2,1536,128]{2,1,0:T(8,128)(2,1)S(1)}, bf16[2,1536,128]{2,1,0:T(8,128)(2,1)S(1)}, u32[]{:S(2)}, u32[]{:S(2)}) %collective-permute-start.2) | collective-permute-done | bytes 786464 | tf_op jit(solution)/shard_map/ppermute | solution.py:32
  101.5 4.0 %collective-permute-done.3.refs_3_ = bf16[2,1536,128]{2,1,0:T(8,128)(2,1)S(1)} collective-permute-done((bf16[2,1536,128]{2,1,0:T(8,128)(2,1)S(1)}, bf16[2,1536,128]{2,1,0:T(8,128)(2,1)S(1)}, u32[]{:S(2)}, u32[]{:S(2)}) %collective-permute-start.3) | collective-permute-done | bytes 786464 | tf_op jit(solution)/shard_map/ppermute | solution.py:32
  105.5 3.0 %collective-permute-start.25 = (bf16[1,1536,128]{2,1,0:T(8,128)(2,1)S(1)}, bf16[1,1536,128]{2,1,0:T(8,128)(2,1)S(1)}, u32[]{:S(2)}, u32[]{:S(2)}) collective-permute-start(bf16[1,1536,128]{2,1,0:T(8,128)(2,1)S(1)} %get-tuple-element.91), channel_id=1, source_target_pairs={{0,16},{8,24},{16,0},{24,8},{32,48},{40,56},{48,32},{56,40},{64,80... | collective-permute-start | bytes 1179656 | tf_op jit(solution)/shard_map/ppermute | solution.py:32
  108.6 5.9 %shard_map.71 = (bf16[1,1536,128]{2,1,0:T(8,128)(2,1)S(1)}, bf16[1,1536,128]{2,1,0:T(8,128)(2,1)S(1)}, bf16[1,1536,128]{2,1,0:T(8,128)(2,1)S(1)}, bf16[1,1536,12...) custom-call(bf16[2,1536,128]{2,1,0:T(8,128)(2,1)S(1)} %collective-pe, ...), custom_call_target="tpu_custom_call", output_to_operand_aliasing={{6}: (5, {}), {7}: (6, {}), {8}: (7, {}), {9}: (8, {})} | custom-call | flops 400000000 | bytes 6291456 | tf_op jit(solution)/shard_map/pallas_call | solution.py:197
  114.7 16.2 %collective-permute-done.24.refs_4_ = bf16[1,1536,128]{2,1,0:T(8,128)(2,1)S(1)} collective-permute-done((bf16[1,1536,128]{2,1,0:T(8,128)(2,1)S(1)}, bf16[1,1536,128]{2,1,0:T(8,128)(2,1)S(1)}, u32[]{:S(2)}, u32[]{:S(2)}) %collective-permute-start.24) | collective-permute-done | bytes 393248 | tf_op jit(solution)/shard_map/ppermute | solution.py:32
  132.1 3.7 %collective-permute-done.10.refs_0_ = bf16[1,1536,128]{2,1,0:T(8,128)(2,1)S(1)} collective-permute-done((bf16[1,1536,128]{2,1,0:T(8,128)(2,1)S(1)}, bf16[1,1536,128]{2,1,0:T(8,128)(2,1)S(1)}, u32[]{:S(2)}, u32[]{:S(2)}) %collective-permute-start.10) | collective-permute-done | bytes 393248 | tf_op jit(solution)/shard_map/ppermute | solution.py:32
  136.8 3.2 %collective-permute-start.19 = (bf16[2,1536,128]{2,1,0:T(8,128)(2,1)S(1)}, bf16[2,1536,128]{2,1,0:T(8,128)(2,1)S(1)}, u32[]{:S(2)}, u32[]{:S(2)}) collective-permute-start(bf16[2,1536,128]{2,1,0:T(8,128)(2,1)S(1)} %get-tuple-element.85), channel_id=1, source_target_pairs={{0,16},{8,24},{16,0},{24,8},{32,48},{40,56},{48,32},{56,40},{64,80... | collective-permute-start | bytes 2359304 | tf_op jit(solution)/shard_map/ppermute | solution.py:32
  140.0 16.9 %collective-permute-done.16.refs_2_ = bf16[2,1536,128]{2,1,0:T(8,128)(2,1)S(1)} collective-permute-done((bf16[2,1536,128]{2,1,0:T(8,128)(2,1)S(1)}, bf16[2,1536,128]{2,1,0:T(8,128)(2,1)S(1)}, u32[]{:S(2)}, u32[]{:S(2)}) %collective-permute-start.16) | collective-permute-done | bytes 786464 | tf_op jit(solution)/shard_map/ppermute | solution.py:32
  156.8 4.2 %collective-permute-start.12 = (bf16[1,1536,128]{2,1,0:T(8,128)(2,1)S(1)}, bf16[1,1536,128]{2,1,0:T(8,128)(2,1)S(1)}, u32[]{:S(2)}, u32[]{:S(2)}) collective-permute-start(bf16[1,1536,128]{2,1,0:T(8,128)(2,1)S(1)} %get-tuple-element.78), channel_id=1, source_target_pairs={{0,96},{8,104},{16,112},{24,120},{32,0},{40,8},{48,16},{56,24},{64... | collective-permute-start | bytes 1179656 | tf_op jit(solution)/shard_map/ppermute | solution.py:32
  161.0 2.7 %collective-permute-start.13 = (bf16[1,1536,128]{2,1,0:T(8,128)(2,1)S(1)}, bf16[1,1536,128]{2,1,0:T(8,128)(2,1)S(1)}, u32[]{:S(2)}, u32[]{:S(2)}) collective-permute-start(bf16[1,1536,128]{2,1,0:T(8,128)(2,1)S(1)} %get-tuple-element.79), channel_id=1, source_target_pairs={{0,24},{8,0},{16,8},{24,16},{32,56},{40,32},{48,40},{56,48},{64,88... | collective-permute-start | bytes 1179656 | tf_op jit(solution)/shard_map/ppermute | solution.py:32
  163.8 1.9 %collective-permute-start.9 = (bf16[1,1536,128]{2,1,0:T(8,128)(2,1)S(1)}, bf16[1,1536,128]{2,1,0:T(8,128)(2,1)S(1)}, u32[]{:S(2)}, u32[]{:S(2)}) collective-permute-start(bf16[1,1536,128]{2,1,0:T(8,128)(2,1)S(1)} %get-tuple-element.75), channel_id=1, source_target_pairs={{0,16},{8,24},{16,0},{24,8},{32,48},{40,56},{48,32},{56,40},{64,80... | collective-permute-start | bytes 1179656 | tf_op jit(solution)/shard_map/ppermute | solution.py:32
  167.3 2.5 %shard_map.73 = (bf16[24576,128]{1,0:T(8,128)(2,1)}, bf16[24576,128]{1,0:T(8,128)(2,1)}, bf16[768,128]{1,0:T(8,128)(2,1)}, bf16[768,128]{1,0:T(8,128)(2,1)}) custom-call(bf16[2,1536,128]{2,1,0:T(8,128)(2,1)S(1)} %collective-permute-done.14.refs_0_, ...), custom_call_target="tpu_custom_call", output_to_operand_aliasing={{0}: (6, {}), {1}: (7, {}), {2}: (8, {}), {3}: (9, {})} | custom-call | flops 600000000 | bytes 9437184 | tf_op jit(solution)/shard_map/pallas_call | solution.py:197
  169.8 3.4 %collective-permute-done.12.refs_2_ = bf16[1,1536,128]{2,1,0:T(8,128)(2,1)S(1)} collective-permute-done((bf16[1,1536,128]{2,1,0:T(8,128)(2,1)S(1)}, bf16[1,1536,128]{2,1,0:T(8,128)(2,1)S(1)}, u32[]{:S(2)}, u32[]{:S(2)}) %collective-permute-start.12) | collective-permute-done | bytes 393248 | tf_op jit(solution)/shard_map/ppermute | solution.py:32
  173.1 3.8 %collective-permute-done.13.refs_3_ = bf16[1,1536,128]{2,1,0:T(8,128)(2,1)S(1)} collective-permute-done((bf16[1,1536,128]{2,1,0:T(8,128)(2,1)S(1)}, bf16[1,1536,128]{2,1,0:T(8,128)(2,1)S(1)}, u32[]{:S(2)}, u32[]{:S(2)}) %collective-permute-start.13) | collective-permute-done | bytes 393248 | tf_op jit(solution)/shard_map/ppermute | solution.py:32
  (38 shorter events, 19.9 us)
Async XLA Ops:
  3.7 62.9 %collective-permute-start.4 = (bf16[4,1536,128]{2,1,0:T(8,128)(2,1)S(1)}, bf16[4,1536,128]{2,1,0:T(8,128)(2,1)S(1)}, u32[]{:S(2)}, u32[]{:S(2)}) collective-permute-start(bf16[4,1536,128]{2,1,0:T(8,128)(2,1)S(1)} %get-tuple-element.62), channel_id=1, source_target_pairs={{0,8},{8,16},{16,24},{24,0},{32,40},{40,48},{48,56},{56,32},{64,72... | collective-permute-start | bytes 4718600 | tf_op jit(solution)/shard_map/ppermute | solution.py:32
  5.5 62.5 %collective-permute-start.5 = (bf16[4,1536,128]{2,1,0:T(8,128)(2,1)S(1)}, bf16[4,1536,128]{2,1,0:T(8,128)(2,1)S(1)}, u32[]{:S(2)}, u32[]{:S(2)}) collective-permute-start(bf16[4,1536,128]{2,1,0:T(8,128)(2,1)S(1)} %get-tuple-element.63), channel_id=1, source_target_pairs={{0,24},{8,0},{16,8},{24,16},{32,56},{40,32},{48,40},{56,48},{64,88... | collective-permute-start | bytes 4718600 | tf_op jit(solution)/shard_map/ppermute | solution.py:32
  7.1 64.0 %collective-permute-start.6 = (bf16[4,1536,128]{2,1,0:T(8,128)(2,1)S(1)}, bf16[4,1536,128]{2,1,0:T(8,128)(2,1)S(1)}, u32[]{:S(2)}, u32[]{:S(2)}) collective-permute-start(bf16[4,1536,128]{2,1,0:T(8,128)(2,1)S(1)} %get-tuple-element.64), channel_id=1, source_target_pairs={{0,32},{8,40},{16,48},{24,56},{32,64},{40,72},{48,80},{56,88},{64,... | collective-permute-start | bytes 4718600 | tf_op jit(solution)/shard_map/ppermute | solution.py:32
  9.1 64.2 %collective-permute-start.7 = (bf16[4,1536,128]{2,1,0:T(8,128)(2,1)S(1)}, bf16[4,1536,128]{2,1,0:T(8,128)(2,1)S(1)}, u32[]{:S(2)}, u32[]{:S(2)}) collective-permute-start(bf16[4,1536,128]{2,1,0:T(8,128)(2,1)S(1)} %get-tuple-element.65), channel_id=1, source_target_pairs={{0,96},{8,104},{16,112},{24,120},{32,0},{40,8},{48,16},{56,24},{64... | collective-permute-start | bytes 4718600 | tf_op jit(solution)/shard_map/ppermute | solution.py:32
  17.9 35.7 %collective-permute-start.20 = (bf16[1,1536,128]{2,1,0:T(8,128)(2,1)S(1)}, bf16[1,1536,128]{2,1,0:T(8,128)(2,1)S(1)}, u32[]{:S(2)}, u32[]{:S(2)}) collective-permute-start(bf16[1,1536,128]{2,1,0:T(8,128)(2,1)S(1)} %get-tuple-element.86), channel_id=1, source_target_pairs={{0,32},{8,40},{16,48},{24,56},{32,64},{40,72},{48,80},{56,88},{64,... | collective-permute-start | bytes 1179656 | tf_op jit(solution)/shard_map/ppermute | solution.py:32
  64.7 21.9 %collective-permute-start = (bf16[2,1536,128]{2,1,0:T(8,128)(2,1)S(1)}, bf16[2,1536,128]{2,1,0:T(8,128)(2,1)S(1)}, u32[]{:S(2)}, u32[]{:S(2)}) collective-permute-start(bf16[2,1536,128]{2,1,0:T(8,128)(2,1)S(1)} %get-tuple-element.58), channel_id=1, source_target_pairs={{0,16},{8,24},{16,0},{24,8},{32,48},{40,56},{48,32},{56,40},{64,80... | collective-permute-start | bytes 2359304 | tf_op jit(solution)/shard_map/ppermute | solution.py:32
  66.6 22.1 %collective-permute-start.1 = (bf16[2,1536,128]{2,1,0:T(8,128)(2,1)S(1)}, bf16[2,1536,128]{2,1,0:T(8,128)(2,1)S(1)}, u32[]{:S(2)}, u32[]{:S(2)}) collective-permute-start(bf16[2,1536,128]{2,1,0:T(8,128)(2,1)S(1)} %get-tuple-element.59), channel_id=1, source_target_pairs={{0,64},{8,72},{16,80},{24,88},{32,96},{40,104},{48,112},{56,120},{... | collective-permute-start | bytes 2359304 | tf_op jit(solution)/shard_map/ppermute | solution.py:32
  68.0 32.4 %collective-permute-start.2 = (bf16[2,1536,128]{2,1,0:T(8,128)(2,1)S(1)}, bf16[2,1536,128]{2,1,0:T(8,128)(2,1)S(1)}, u32[]{:S(2)}, u32[]{:S(2)}) collective-permute-start(bf16[2,1536,128]{2,1,0:T(8,128)(2,1)S(1)} %get-tuple-element.60), channel_id=1, source_target_pairs={{0,16},{8,24},{16,0},{24,8},{32,48},{40,56},{48,32},{56,40},{64,80... | collective-permute-start | bytes 2359304 | tf_op jit(solution)/shard_map/ppermute | solution.py:32
  71.1 34.5 %collective-permute-start.3 = (bf16[2,1536,128]{2,1,0:T(8,128)(2,1)S(1)}, bf16[2,1536,128]{2,1,0:T(8,128)(2,1)S(1)}, u32[]{:S(2)}, u32[]{:S(2)}) collective-permute-start(bf16[2,1536,128]{2,1,0:T(8,128)(2,1)S(1)} %get-tuple-element.61), channel_id=1, source_target_pairs={{0,64},{8,72},{16,80},{24,88},{32,96},{40,104},{48,112},{56,120},{... | collective-permute-start | bytes 2359304 | tf_op jit(solution)/shard_map/ppermute | solution.py:32
  73.3 41.2 %collective-permute-start.22 = (bf16[1,1536,128]{2,1,0:T(8,128)(2,1)S(1)}, bf16[1,1536,128]{2,1,0:T(8,128)(2,1)S(1)}, u32[]{:S(2)}, u32[]{:S(2)}) collective-permute-start(bf16[1,1536,128]{2,1,0:T(8,128)(2,1)S(1)} %get-tuple-element.88), channel_id=1, source_target_pairs={{0,96},{8,104},{16,112},{24,120},{32,0},{40,8},{48,16},{56,24},{64... | collective-permute-start | bytes 1179656 | tf_op jit(solution)/shard_map/ppermute | solution.py:32
  86.6 50.2 %collective-permute-start.14 = (bf16[2,1536,128]{2,1,0:T(8,128)(2,1)S(1)}, bf16[2,1536,128]{2,1,0:T(8,128)(2,1)S(1)}, u32[]{:S(2)}, u32[]{:S(2)}) collective-permute-start(bf16[2,1536,128]{2,1,0:T(8,128)(2,1)S(1)} %get-tuple-element.80), channel_id=1, source_target_pairs={{0,32},{8,40},{16,48},{24,56},{32,64},{40,72},{48,80},{56,88},{64,... | collective-permute-start | bytes 2359304 | tf_op jit(solution)/shard_map/ppermute | solution.py:32
  88.7 25.9 %collective-permute-start.23 = (bf16[1,1536,128]{2,1,0:T(8,128)(2,1)S(1)}, bf16[1,1536,128]{2,1,0:T(8,128)(2,1)S(1)}, u32[]{:S(2)}, u32[]{:S(2)}) collective-permute-start(bf16[1,1536,128]{2,1,0:T(8,128)(2,1)S(1)} %get-tuple-element.89), channel_id=1, source_target_pairs={{0,24},{8,0},{16,8},{24,16},{32,56},{40,32},{48,40},{56,48},{64,88... | collective-permute-start | bytes 1179656 | tf_op jit(solution)/shard_map/ppermute | solution.py:32
  100.5 30.4 %collective-permute-start.24 = (bf16[1,1536,128]{2,1,0:T(8,128)(2,1)S(1)}, bf16[1,1536,128]{2,1,0:T(8,128)(2,1)S(1)}, u32[]{:S(2)}, u32[]{:S(2)}) collective-permute-start(bf16[1,1536,128]{2,1,0:T(8,128)(2,1)S(1)} %get-tuple-element.90), channel_id=1, source_target_pairs={{0,64},{8,72},{16,80},{24,88},{32,96},{40,104},{48,112},{56,120},{... | collective-permute-start | bytes 1179656 | tf_op jit(solution)/shard_map/ppermute | solution.py:32
  105.5 25.3 %collective-permute-start.25 = (bf16[1,1536,128]{2,1,0:T(8,128)(2,1)S(1)}, bf16[1,1536,128]{2,1,0:T(8,128)(2,1)S(1)}, u32[]{:S(2)}, u32[]{:S(2)}) collective-permute-start(bf16[1,1536,128]{2,1,0:T(8,128)(2,1)S(1)} %get-tuple-element.91), channel_id=1, source_target_pairs={{0,16},{8,24},{16,0},{24,8},{32,48},{40,56},{48,32},{56,40},{64,80... | collective-permute-start | bytes 1179656 | tf_op jit(solution)/shard_map/ppermute | solution.py:32
  114.5 21.3 %collective-permute-start.10 = (bf16[1,1536,128]{2,1,0:T(8,128)(2,1)S(1)}, bf16[1,1536,128]{2,1,0:T(8,128)(2,1)S(1)}, u32[]{:S(2)}, u32[]{:S(2)}) collective-permute-start(bf16[1,1536,128]{2,1,0:T(8,128)(2,1)S(1)} %get-tuple-element.76), channel_id=1, source_target_pairs={{0,32},{8,40},{16,48},{24,56},{32,64},{40,72},{48,80},{56,88},{64,... | collective-permute-start | bytes 1179656 | tf_op jit(solution)/shard_map/ppermute | solution.py:32
  114.6 25.4 %collective-permute-start.15 = (bf16[2,1536,128]{2,1,0:T(8,128)(2,1)S(1)}, bf16[2,1536,128]{2,1,0:T(8,128)(2,1)S(1)}, u32[]{:S(2)}, u32[]{:S(2)}) collective-permute-start(bf16[2,1536,128]{2,1,0:T(8,128)(2,1)S(1)} %get-tuple-element.81), channel_id=1, source_target_pairs={{0,8},{8,16},{16,24},{24,0},{32,40},{40,48},{48,56},{56,32},{64,72... | collective-permute-start | bytes 2359304 | tf_op jit(solution)/shard_map/ppermute | solution.py:32
  130.8 26.0 %collective-permute-start.16 = (bf16[2,1536,128]{2,1,0:T(8,128)(2,1)S(1)}, bf16[2,1536,128]{2,1,0:T(8,128)(2,1)S(1)}, u32[]{:S(2)}, u32[]{:S(2)}) collective-permute-start(bf16[2,1536,128]{2,1,0:T(8,128)(2,1)S(1)} %get-tuple-element.82), channel_id=1, source_target_pairs={{0,96},{8,104},{16,112},{24,120},{32,0},{40,8},{48,16},{56,24},{64... | collective-permute-start | bytes 2359304 | tf_op jit(solution)/shard_map/ppermute | solution.py:32
  130.9 30.2 %collective-permute-start.17 = (bf16[2,1536,128]{2,1,0:T(8,128)(2,1)S(1)}, bf16[2,1536,128]{2,1,0:T(8,128)(2,1)S(1)}, u32[]{:S(2)}, u32[]{:S(2)}) collective-permute-start(bf16[2,1536,128]{2,1,0:T(8,128)(2,1)S(1)} %get-tuple-element.83), channel_id=1, source_target_pairs={{0,24},{8,0},{16,8},{24,16},{32,56},{40,32},{48,40},{56,48},{64,88... | collective-permute-start | bytes 2359304 | tf_op jit(solution)/shard_map/ppermute | solution.py:32
  135.8 28.0 %collective-permute-start.18 = (bf16[2,1536,128]{2,1,0:T(8,128)(2,1)S(1)}, bf16[2,1536,128]{2,1,0:T(8,128)(2,1)S(1)}, u32[]{:S(2)}, u32[]{:S(2)}) collective-permute-start(bf16[2,1536,128]{2,1,0:T(8,128)(2,1)S(1)} %get-tuple-element.84), channel_id=1, source_target_pairs={{0,64},{8,72},{16,80},{24,88},{32,96},{40,104},{48,112},{56,120},{... | collective-permute-start | bytes 2359304 | tf_op jit(solution)/shard_map/ppermute | solution.py:32
  136.8 27.0 %collective-permute-start.19 = (bf16[2,1536,128]{2,1,0:T(8,128)(2,1)S(1)}, bf16[2,1536,128]{2,1,0:T(8,128)(2,1)S(1)}, u32[]{:S(2)}, u32[]{:S(2)}) collective-permute-start(bf16[2,1536,128]{2,1,0:T(8,128)(2,1)S(1)} %get-tuple-element.85), channel_id=1, source_target_pairs={{0,16},{8,24},{16,0},{24,8},{32,48},{40,56},{48,32},{56,40},{64,80... | collective-permute-start | bytes 2359304 | tf_op jit(solution)/shard_map/ppermute | solution.py:32
  140.0 29.8 %collective-permute-start.11 = (bf16[1,1536,128]{2,1,0:T(8,128)(2,1)S(1)}, bf16[1,1536,128]{2,1,0:T(8,128)(2,1)S(1)}, u32[]{:S(2)}, u32[]{:S(2)}) collective-permute-start(bf16[1,1536,128]{2,1,0:T(8,128)(2,1)S(1)} %get-tuple-element.77), channel_id=1, source_target_pairs={{0,8},{8,16},{16,24},{24,0},{32,40},{40,48},{48,56},{56,32},{64,72... | collective-permute-start | bytes 1179656 | tf_op jit(solution)/shard_map/ppermute | solution.py:32
  156.8 16.3 %collective-permute-start.12 = (bf16[1,1536,128]{2,1,0:T(8,128)(2,1)S(1)}, bf16[1,1536,128]{2,1,0:T(8,128)(2,1)S(1)}, u32[]{:S(2)}, u32[]{:S(2)}) collective-permute-start(bf16[1,1536,128]{2,1,0:T(8,128)(2,1)S(1)} %get-tuple-element.78), channel_id=1, source_target_pairs={{0,96},{8,104},{16,112},{24,120},{32,0},{40,8},{48,16},{56,24},{64... | collective-permute-start | bytes 1179656 | tf_op jit(solution)/shard_map/ppermute | solution.py:32
  161.0 15.9 %collective-permute-start.13 = (bf16[1,1536,128]{2,1,0:T(8,128)(2,1)S(1)}, bf16[1,1536,128]{2,1,0:T(8,128)(2,1)S(1)}, u32[]{:S(2)}, u32[]{:S(2)}) collective-permute-start(bf16[1,1536,128]{2,1,0:T(8,128)(2,1)S(1)} %get-tuple-element.79), channel_id=1, source_target_pairs={{0,24},{8,0},{16,8},{24,16},{32,56},{40,32},{48,40},{56,48},{64,88... | collective-permute-start | bytes 1179656 | tf_op jit(solution)/shard_map/ppermute | solution.py:32
  163.8 14.5 %collective-permute-start.9 = (bf16[1,1536,128]{2,1,0:T(8,128)(2,1)S(1)}, bf16[1,1536,128]{2,1,0:T(8,128)(2,1)S(1)}, u32[]{:S(2)}, u32[]{:S(2)}) collective-permute-start(bf16[1,1536,128]{2,1,0:T(8,128)(2,1)S(1)} %get-tuple-element.75), channel_id=1, source_target_pairs={{0,16},{8,24},{16,0},{24,8},{32,48},{40,56},{48,32},{56,40},{64,80... | collective-permute-start | bytes 1179656 | tf_op jit(solution)/shard_map/ppermute | solution.py:32
  (2 other events, 25.5 us)

commit v4 on v3

--- a/solution.py
+++ b/solution.py
@@ -30,22 +30,6 @@
 def shift(a, dy, dz):
     pairs = [(i, slot(i % SIDE + dy, i // SIDE + dz)) for i in range(SIDE * SIDE)]
     return lax.ppermute(a, SEQ, pairs)
-
-
-def cos_sin(a):
-    j = jnp.floor(a * 0.636619772367581 + 0.5)
-    r = a - j * 1.5703125
-    r = r - j * 4.837512969970703e-4
-    r = r - j * 7.549789948768648e-8
-    z = r * r
-    s = r + r * z * (-1.6666654611e-1 + z * (8.3321608736e-3 + z * -1.9515295891e-4))
-    c = 1.0 - 0.5 * z + z * z * (4.166664568298827e-2 + z * (-1.388731625493765e-3 + z * 2.443315711809948e-5))
-    odd = jnp.abs(j) == 1.0
-    near_c = jnp.where(odd, s, c)
-    near_s = jnp.where(odd, c, s)
-    cosine = jnp.where(j == 0.0, near_c, jnp.where(j == -1.0, near_c, -near_c))
-    sine = jnp.where(j == 0.0, near_s, jnp.where(j == 1.0, near_s, -near_s))
-    return cosine, sine
 
 
 class Task(NamedTuple):
@@ -94,7 +78,8 @@
 
         def spread(q, _, t=t):
             lanes = pl.ds(pl.multiple_of(q * 128, 128), 128)
-            c, s = cos_sin(raw_angle[t, :, lanes])
+            a = raw_angle[t, :, lanes]
+            c, s = jnp.cos(a), jnp.sin(a)
             wide_c[t, lanes, :] = jnp.concatenate([c, c], axis=0).T
             wide_s[t, lanes, :] = jnp.concatenate([-s, s], axis=0).T
             return 0

time: 180 us -> 180 us (level)
  waiting for transfers between devices: 107 us -> 102 us
  Pallas kernels: 35.1 us -> 39.3 us
    ppermute x26, waiting for transfers between devices: 107 us -> 102 us  [shift(): return lax.ppermute(a, SEQ, pairs)]
    pallas_call x10, Pallas kernels: 35.1 us -> 39.3 us  [step(): pl.pallas_call(functools.partial(step_kernel, len(far), len(near), len(ou...]
  transfers between devices with their start and end apart: 26 -> 26, of which waited for: 11 -> 10; matrix products, arithmetic and copies ran while one was open for 0% -> 0% of each run, Pallas kernels for 17% -> 20%
where the time goes in v4:
time: 180 us; the launch traced here: 179 us
  waiting for transfers between devices  102 us (57%)
  Pallas kernels  39.3 us (22%)
  starting transfers between devices  36.7 us (20%)
    ppermute x26, waiting for transfers between devices, shift(): return lax.ppermute(a, SEQ, pairs)  102 us
    pallas_call x10, Pallas kernels, step(): pl.pallas_call(functools.partial(step_kernel, len(far), len(near), len(ou...  39.3 us
    ppermute x26, starting transfers between devices, shift(): return lax.ppermute(a, SEQ, pairs)  36.7 us
  transfers between devices with their start and end apart: 26, of which 10 were waited for; matrix products, arithmetic and copies ran while one was open for 0% of the time, Pallas kernels for 20%

profile of v4, /device:TPU:0, one launch (start us, length us, event | category | flops | bytes accessed | tf_op | source)
XLA Modules:
  0.0 179.2 jit_solution(6461423873709061647)
XLA Ops:
  0.6 3.1 %shard_map.68 = (bf16[4,1536,128]{2,1,0:T(8,128)(2,1)S(1)}, bf16[4,1536,128]{2,1,0:T(8,128)(2,1)S(1)}, bf16[4,1536,128]{2,1,0:T(8,128)(2,1)S(1)}, bf16[4,1536,128]{2,1,0:T(8,128)(2,1)S(1)}) custom-call(bf16[16,1536,128]{2,1,0:T(8,128)(2,1)} %bitcast.9, bf16[16,1536,128]{2,1,0:T(8,128)(2,1)} %bitcast.13), custom_call_target="tpu_custom_call" | custom-call | flops 800000000 | bytes 12582912 | tf_op jit(solution)/shard_map/pallas_call | solution.py:182
  3.7 1.8 collective-permute-start.4
  7.1 2.0 %collective-permute-start.6 = (bf16[4,1536,128]{2,1,0:T(8,128)(2,1)S(1)}, bf16[4,1536,128]{2,1,0:T(8,128)(2,1)S(1)}, u32[]{:S(2)}, u32[]{:S(2)}) collective-permute-start(bf16[4,1536,128]{2,1,0:T(8,128)(2,1)S(1)} %get-tuple-element.64), channel_id=1, source_target_pairs={{0,32},{8,40},{16,48},{24,56},{32,64},{40,72},{48,80},{56,88},{64,... | collective-permute-start | bytes 4718600 | tf_op jit(solution)/shard_map/ppermute | solution.py:32
  9.1 2.1 %collective-permute-start.7 = (bf16[4,1536,128]{2,1,0:T(8,128)(2,1)S(1)}, bf16[4,1536,128]{2,1,0:T(8,128)(2,1)S(1)}, u32[]{:S(2)}, u32[]{:S(2)}) collective-permute-start(bf16[4,1536,128]{2,1,0:T(8,128)(2,1)S(1)} %get-tuple-element.65), channel_id=1, source_target_pairs={{0,96},{8,104},{16,112},{24,120},{32,0},{40,8},{48,16},{56,24},{64... | collective-permute-start | bytes 4718600 | tf_op jit(solution)/shard_map/ppermute | solution.py:32
  11.2 7.7 %shard_map.69 = (bf16[1,1536,128]{2,1,0:T(8,128)(2,1)S(1)}, bf16[1,1536,128]{2,1,0:T(8,128)(2,1)S(1)}, bf16[1,1536,128]{2,1,0:T(8,128)(2,1)S(1)}, bf16[1,1536,12...) custom-call(bf16[16,1536,128]{2,1,0:T(8,128)(2,1)} %bitcast.10, ...), custom_call_target="tpu_custom_call" | custom-call | flops 400000000 | bytes 6291456 | tf_op jit(solution)/shard_map/pallas_call | solution.py:182
  19.0 34.6 %collective-permute-done.20.refs_0_ = bf16[1,1536,128]{2,1,0:T(8,128)(2,1)S(1)} collective-permute-done((bf16[1,1536,128]{2,1,0:T(8,128)(2,1)S(1)}, bf16[1,1536,128]{2,1,0:T(8,128)(2,1)S(1)}, u32[]{:S(2)}, u32[]{:S(2)}) %collective-permute-start.20) | collective-permute-done | bytes 393248 | tf_op jit(solution)/shard_map/ppermute | solution.py:32
  55.3 9.4 %collective-permute-done.21.refs_1_ = bf16[1,1536,128]{2,1,0:T(8,128)(2,1)S(1)} collective-permute-done((bf16[1,1536,128]{2,1,0:T(8,128)(2,1)S(1)}, bf16[1,1536,128]{2,1,0:T(8,128)(2,1)S(1)}, u32[]{:S(2)}, u32[]{:S(2)}) %collective-permute-start.21) | collective-permute-done | bytes 393248 | tf_op jit(solution)/shard_map/ppermute | solution.py:32
  68.0 3.0 %collective-permute-start.2 = (bf16[2,1536,128]{2,1,0:T(8,128)(2,1)S(1)}, bf16[2,1536,128]{2,1,0:T(8,128)(2,1)S(1)}, u32[]{:S(2)}, u32[]{:S(2)}) collective-permute-start(bf16[2,1536,128]{2,1,0:T(8,128)(2,1)S(1)} %get-tuple-element.60), channel_id=1, source_target_pairs={{0,16},{8,24},{16,0},{24,8},{32,48},{40,56},{48,32},{56,40},{64,80... | collective-permute-start | bytes 2359304 | tf_op jit(solution)/shard_map/ppermute | solution.py:32
  71.1 2.2 %collective-permute-start.3 = (bf16[2,1536,128]{2,1,0:T(8,128)(2,1)S(1)}, bf16[2,1536,128]{2,1,0:T(8,128)(2,1)S(1)}, u32[]{:S(2)}, u32[]{:S(2)}) collective-permute-start(bf16[2,1536,128]{2,1,0:T(8,128)(2,1)S(1)} %get-tuple-element.61), channel_id=1, source_target_pairs={{0,64},{8,72},{16,80},{24,88},{32,96},{40,104},{48,112},{56,120},{... | collective-permute-start | bytes 2359304 | tf_op jit(solution)/shard_map/ppermute | solution.py:32
  74.7 12.3 %shard_map.70 = (bf16[2,1536,128]{2,1,0:T(8,128)(2,1)S(1)}, bf16[2,1536,128]{2,1,0:T(8,128)(2,1)S(1)}, bf16[2,1536,128]{2,1,0:T(8,128)(2,1)S(1)}, bf16[2,1536,12...) custom-call(bf16[4,1536,128]{2,1,0:T(8,128)(2,1)S(1)} %collective-pe, ...), custom_call_target="tpu_custom_call", output_to_operand_aliasing={{6}: (5, {}), {7}: (6, {}), {8}: (7, {}), {9}: (8, {})} | custom-call | flops 800000000 | bytes 12582912 | tf_op jit(solution)/shard_map/pallas_call | solution.py:182
  90.0 10.5 %collective-permute-done.2.refs_2_ = bf16[2,1536,128]{2,1,0:T(8,128)(2,1)S(1)} collective-permute-done((bf16[2,1536,128]{2,1,0:T(8,128)(2,1)S(1)}, bf16[2,1536,128]{2,1,0:T(8,128)(2,1)S(1)}, u32[]{:S(2)}, u32[]{:S(2)}) %collective-permute-start.2) | collective-permute-done | bytes 786464 | tf_op jit(solution)/shard_map/ppermute | solution.py:32
  101.5 4.0 %collective-permute-done.3.refs_3_ = bf16[2,1536,128]{2,1,0:T(8,128)(2,1)S(1)} collective-permute-done((bf16[2,1536,128]{2,1,0:T(8,128)(2,1)S(1)}, bf16[2,1536,128]{2,1,0:T(8,128)(2,1)S(1)}, u32[]{:S(2)}, u32[]{:S(2)}) %collective-permute-start.3) | collective-permute-done | bytes 786464 | tf_op jit(solution)/shard_map/ppermute | solution.py:32
  105.5 3.0 %collective-permute-start.25 = (bf16[1,1536,128]{2,1,0:T(8,128)(2,1)S(1)}, bf16[1,1536,128]{2,1,0:T(8,128)(2,1)S(1)}, u32[]{:S(2)}, u32[]{:S(2)}) collective-permute-start(bf16[1,1536,128]{2,1,0:T(8,128)(2,1)S(1)} %get-tuple-element.91), channel_id=1, source_target_pairs={{0,16},{8,24},{16,0},{24,8},{32,48},{40,56},{48,32},{56,40},{64,80... | collective-permute-start | bytes 1179656 | tf_op jit(solution)/shard_map/ppermute | solution.py:32
  108.6 7.0 %shard_map.71 = (bf16[1,1536,128]{2,1,0:T(8,128)(2,1)S(1)}, bf16[1,1536,128]{2,1,0:T(8,128)(2,1)S(1)}, bf16[1,1536,128]{2,1,0:T(8,128)(2,1)S(1)}, bf16[1,1536,12...) custom-call(bf16[2,1536,128]{2,1,0:T(8,128)(2,1)S(1)} %collective-pe, ...), custom_call_target="tpu_custom_call", output_to_operand_aliasing={{6}: (5, {}), {7}: (6, {}), {8}: (7, {}), {9}: (8, {})} | custom-call | flops 400000000 | bytes 6291456 | tf_op jit(solution)/shard_map/pallas_call | solution.py:182
  115.7 15.1 %collective-permute-done.24.refs_4_ = bf16[1,1536,128]{2,1,0:T(8,128)(2,1)S(1)} collective-permute-done((bf16[1,1536,128]{2,1,0:T(8,128)(2,1)S(1)}, bf16[1,1536,128]{2,1,0:T(8,128)(2,1)S(1)}, u32[]{:S(2)}, u32[]{:S(2)}) %collective-permute-start.24) | collective-permute-done | bytes 393248 | tf_op jit(solution)/shard_map/ppermute | solution.py:32
  132.1 3.7 %collective-permute-done.10.refs_0_ = bf16[1,1536,128]{2,1,0:T(8,128)(2,1)S(1)} collective-permute-done((bf16[1,1536,128]{2,1,0:T(8,128)(2,1)S(1)}, bf16[1,1536,128]{2,1,0:T(8,128)(2,1)S(1)}, u32[]{:S(2)}, u32[]{:S(2)}) %collective-permute-start.10) | collective-permute-done | bytes 393248 | tf_op jit(solution)/shard_map/ppermute | solution.py:32
  136.8 3.2 %collective-permute-start.19 = (bf16[2,1536,128]{2,1,0:T(8,128)(2,1)S(1)}, bf16[2,1536,128]{2,1,0:T(8,128)(2,1)S(1)}, u32[]{:S(2)}, u32[]{:S(2)}) collective-permute-start(bf16[2,1536,128]{2,1,0:T(8,128)(2,1)S(1)} %get-tuple-element.85), channel_id=1, source_target_pairs={{0,16},{8,24},{16,0},{24,8},{32,48},{40,56},{48,32},{56,40},{64,80... | collective-permute-start | bytes 2359304 | tf_op jit(solution)/shard_map/ppermute | solution.py:32
  140.0 16.9 %collective-permute-done.16.refs_2_ = bf16[2,1536,128]{2,1,0:T(8,128)(2,1)S(1)} collective-permute-done((bf16[2,1536,128]{2,1,0:T(8,128)(2,1)S(1)}, bf16[2,1536,128]{2,1,0:T(8,128)(2,1)S(1)}, u32[]{:S(2)}, u32[]{:S(2)}) %collective-permute-start.16) | collective-permute-done | bytes 786464 | tf_op jit(solution)/shard_map/ppermute | solution.py:32
  156.8 4.2 %collective-permute-start.12 = (bf16[1,1536,128]{2,1,0:T(8,128)(2,1)S(1)}, bf16[1,1536,128]{2,1,0:T(8,128)(2,1)S(1)}, u32[]{:S(2)}, u32[]{:S(2)}) collective-permute-start(bf16[1,1536,128]{2,1,0:T(8,128)(2,1)S(1)} %get-tuple-element.78), channel_id=1, source_target_pairs={{0,96},{8,104},{16,112},{24,120},{32,0},{40,8},{48,16},{56,24},{64... | collective-permute-start | bytes 1179656 | tf_op jit(solution)/shard_map/ppermute | solution.py:32
  161.0 2.7 %collective-permute-start.13 = (bf16[1,1536,128]{2,1,0:T(8,128)(2,1)S(1)}, bf16[1,1536,128]{2,1,0:T(8,128)(2,1)S(1)}, u32[]{:S(2)}, u32[]{:S(2)}) collective-permute-start(bf16[1,1536,128]{2,1,0:T(8,128)(2,1)S(1)} %get-tuple-element.79), channel_id=1, source_target_pairs={{0,24},{8,0},{16,8},{24,16},{32,56},{40,32},{48,40},{56,48},{64,88... | collective-permute-start | bytes 1179656 | tf_op jit(solution)/shard_map/ppermute | solution.py:32
  163.8 1.9 %collective-permute-start.9 = (bf16[1,1536,128]{2,1,0:T(8,128)(2,1)S(1)}, bf16[1,1536,128]{2,1,0:T(8,128)(2,1)S(1)}, u32[]{:S(2)}, u32[]{:S(2)}) collective-permute-start(bf16[1,1536,128]{2,1,0:T(8,128)(2,1)S(1)} %get-tuple-element.75), channel_id=1, source_target_pairs={{0,16},{8,24},{16,0},{24,8},{32,48},{40,56},{48,32},{56,40},{64,80... | collective-permute-start | bytes 1179656 | tf_op jit(solution)/shard_map/ppermute | solution.py:32
  167.3 2.5 %shard_map.73 = (bf16[24576,128]{1,0:T(8,128)(2,1)}, bf16[24576,128]{1,0:T(8,128)(2,1)}, bf16[768,128]{1,0:T(8,128)(2,1)}, bf16[768,128]{1,0:T(8,128)(2,1)}) custom-call(bf16[2,1536,128]{2,1,0:T(8,128)(2,1)S(1)} %collective-permute-done.14.refs_0_, ...), custom_call_target="tpu_custom_call", output_to_operand_aliasing={{0}: (6, {}), {1}: (7, {}), {2}: (8, {}), {3}: (9, {})} | custom-call | flops 600000000 | bytes 9437184 | tf_op jit(solution)/shard_map/pallas_call | solution.py:182
  169.8 3.4 %collective-permute-done.12.refs_2_ = bf16[1,1536,128]{2,1,0:T(8,128)(2,1)S(1)} collective-permute-done((bf16[1,1536,128]{2,1,0:T(8,128)(2,1)S(1)}, bf16[1,1536,128]{2,1,0:T(8,128)(2,1)S(1)}, u32[]{:S(2)}, u32[]{:S(2)}) %collective-permute-start.12) | collective-permute-done | bytes 393248 | tf_op jit(solution)/shard_map/ppermute | solution.py:32
  173.1 3.8 %collective-permute-done.13.refs_3_ = bf16[1,1536,128]{2,1,0:T(8,128)(2,1)S(1)} collective-permute-done((bf16[1,1536,128]{2,1,0:T(8,128)(2,1)S(1)}, bf16[1,1536,128]{2,1,0:T(8,128)(2,1)S(1)}, u32[]{:S(2)}, u32[]{:S(2)}) %collective-permute-start.13) | collective-permute-done | bytes 393248 | tf_op jit(solution)/shard_map/ppermute | solution.py:32
  (38 shorter events, 18.2 us)
Async XLA Ops:
  3.7 62.9 %collective-permute-start.4 = (bf16[4,1536,128]{2,1,0:T(8,128)(2,1)S(1)}, bf16[4,1536,128]{2,1,0:T(8,128)(2,1)S(1)}, u32[]{:S(2)}, u32[]{:S(2)}) collective-permute-start(bf16[4,1536,128]{2,1,0:T(8,128)(2,1)S(1)} %get-tuple-element.62), channel_id=1, source_target_pairs={{0,8},{8,16},{16,24},{24,0},{32,40},{40,48},{48,56},{56,32},{64,72... | collective-permute-start | bytes 4718600 | tf_op jit(solution)/shard_map/ppermute | solution.py:32
  5.5 62.5 %collective-permute-start.5 = (bf16[4,1536,128]{2,1,0:T(8,128)(2,1)S(1)}, bf16[4,1536,128]{2,1,0:T(8,128)(2,1)S(1)}, u32[]{:S(2)}, u32[]{:S(2)}) collective-permute-start(bf16[4,1536,128]{2,1,0:T(8,128)(2,1)S(1)} %get-tuple-element.63), channel_id=1, source_target_pairs={{0,24},{8,0},{16,8},{24,16},{32,56},{40,32},{48,40},{56,48},{64,88... | collective-permute-start | bytes 4718600 | tf_op jit(solution)/shard_map/ppermute | solution.py:32
  7.1 64.0 %collective-permute-start.6 = (bf16[4,1536,128]{2,1,0:T(8,128)(2,1)S(1)}, bf16[4,1536,128]{2,1,0:T(8,128)(2,1)S(1)}, u32[]{:S(2)}, u32[]{:S(2)}) collective-permute-start(bf16[4,1536,128]{2,1,0:T(8,128)(2,1)S(1)} %get-tuple-element.64), channel_id=1, source_target_pairs={{0,32},{8,40},{16,48},{24,56},{32,64},{40,72},{48,80},{56,88},{64,... | collective-permute-start | bytes 4718600 | tf_op jit(solution)/shard_map/ppermute | solution.py:32
  9.1 64.2 %collective-permute-start.7 = (bf16[4,1536,128]{2,1,0:T(8,128)(2,1)S(1)}, bf16[4,1536,128]{2,1,0:T(8,128)(2,1)S(1)}, u32[]{:S(2)}, u32[]{:S(2)}) collective-permute-start(bf16[4,1536,128]{2,1,0:T(8,128)(2,1)S(1)} %get-tuple-element.65), channel_id=1, source_target_pairs={{0,96},{8,104},{16,112},{24,120},{32,0},{40,8},{48,16},{56,24},{64... | collective-permute-start | bytes 4718600 | tf_op jit(solution)/shard_map/ppermute | solution.py:32
  18.9 34.7 %collective-permute-start.20 = (bf16[1,1536,128]{2,1,0:T(8,128)(2,1)S(1)}, bf16[1,1536,128]{2,1,0:T(8,128)(2,1)S(1)}, u32[]{:S(2)}, u32[]{:S(2)}) collective-permute-start(bf16[1,1536,128]{2,1,0:T(8,128)(2,1)S(1)} %get-tuple-element.86), channel_id=1, source_target_pairs={{0,32},{8,40},{16,48},{24,56},{32,64},{40,72},{48,80},{56,88},{64,... | collective-permute-start | bytes 1179656 | tf_op jit(solution)/shard_map/ppermute | solution.py:32
  64.7 22.4 %collective-permute-start = (bf16[2,1536,128]{2,1,0:T(8,128)(2,1)S(1)}, bf16[2,1536,128]{2,1,0:T(8,128)(2,1)S(1)}, u32[]{:S(2)}, u32[]{:S(2)}) collective-permute-start(bf16[2,1536,128]{2,1,0:T(8,128)(2,1)S(1)} %get-tuple-element.58), channel_id=1, source_target_pairs={{0,16},{8,24},{16,0},{24,8},{32,48},{40,56},{48,32},{56,40},{64,80... | collective-permute-start | bytes 2359304 | tf_op jit(solution)/shard_map/ppermute | solution.py:32
  66.6 22.1 %collective-permute-start.1 = (bf16[2,1536,128]{2,1,0:T(8,128)(2,1)S(1)}, bf16[2,1536,128]{2,1,0:T(8,128)(2,1)S(1)}, u32[]{:S(2)}, u32[]{:S(2)}) collective-permute-start(bf16[2,1536,128]{2,1,0:T(8,128)(2,1)S(1)} %get-tuple-element.59), channel_id=1, source_target_pairs={{0,64},{8,72},{16,80},{24,88},{32,96},{40,104},{48,112},{56,120},{... | collective-permute-start | bytes 2359304 | tf_op jit(solution)/shard_map/ppermute | solution.py:32
  68.0 32.4 %collective-permute-start.2 = (bf16[2,1536,128]{2,1,0:T(8,128)(2,1)S(1)}, bf16[2,1536,128]{2,1,0:T(8,128)(2,1)S(1)}, u32[]{:S(2)}, u32[]{:S(2)}) collective-permute-start(bf16[2,1536,128]{2,1,0:T(8,128)(2,1)S(1)} %get-tuple-element.60), channel_id=1, source_target_pairs={{0,16},{8,24},{16,0},{24,8},{32,48},{40,56},{48,32},{56,40},{64,80... | collective-permute-start | bytes 2359304 | tf_op jit(solution)/shard_map/ppermute | solution.py:32
  71.1 34.5 %collective-permute-start.3 = (bf16[2,1536,128]{2,1,0:T(8,128)(2,1)S(1)}, bf16[2,1536,128]{2,1,0:T(8,128)(2,1)S(1)}, u32[]{:S(2)}, u32[]{:S(2)}) collective-permute-start(bf16[2,1536,128]{2,1,0:T(8,128)(2,1)S(1)} %get-tuple-element.61), channel_id=1, source_target_pairs={{0,64},{8,72},{16,80},{24,88},{32,96},{40,104},{48,112},{56,120},{... | collective-permute-start | bytes 2359304 | tf_op jit(solution)/shard_map/ppermute | solution.py:32
  73.3 42.2 %collective-permute-start.22 = (bf16[1,1536,128]{2,1,0:T(8,128)(2,1)S(1)}, bf16[1,1536,128]{2,1,0:T(8,128)(2,1)S(1)}, u32[]{:S(2)}, u32[]{:S(2)}) collective-permute-start(bf16[1,1536,128]{2,1,0:T(8,128)(2,1)S(1)} %get-tuple-element.88), channel_id=1, source_target_pairs={{0,96},{8,104},{16,112},{24,120},{32,0},{40,8},{48,16},{56,24},{64... | collective-permute-start | bytes 1179656 | tf_op jit(solution)/shard_map/ppermute | solution.py:32
  87.1 49.7 %collective-permute-start.14 = (bf16[2,1536,128]{2,1,0:T(8,128)(2,1)S(1)}, bf16[2,1536,128]{2,1,0:T(8,128)(2,1)S(1)}, u32[]{:S(2)}, u32[]{:S(2)}) collective-permute-start(bf16[2,1536,128]{2,1,0:T(8,128)(2,1)S(1)} %get-tuple-element.80), channel_id=1, source_target_pairs={{0,32},{8,40},{16,48},{24,56},{32,64},{40,72},{48,80},{56,88},{64,... | collective-permute-start | bytes 2359304 | tf_op jit(solution)/shard_map/ppermute | solution.py:32
  88.7 26.9 %collective-permute-start.23 = (bf16[1,1536,128]{2,1,0:T(8,128)(2,1)S(1)}, bf16[1,1536,128]{2,1,0:T(8,128)(2,1)S(1)}, u32[]{:S(2)}, u32[]{:S(2)}) collective-permute-start(bf16[1,1536,128]{2,1,0:T(8,128)(2,1)S(1)} %get-tuple-element.89), channel_id=1, source_target_pairs={{0,24},{8,0},{16,8},{24,16},{32,56},{40,32},{48,40},{56,48},{64,88... | collective-permute-start | bytes 1179656 | tf_op jit(solution)/shard_map/ppermute | solution.py:32
  100.5 30.4 %collective-permute-start.24 = (bf16[1,1536,128]{2,1,0:T(8,128)(2,1)S(1)}, bf16[1,1536,128]{2,1,0:T(8,128)(2,1)S(1)}, u32[]{:S(2)}, u32[]{:S(2)}) collective-permute-start(bf16[1,1536,128]{2,1,0:T(8,128)(2,1)S(1)} %get-tuple-element.90), channel_id=1, source_target_pairs={{0,64},{8,72},{16,80},{24,88},{32,96},{40,104},{48,112},{56,120},{... | collective-permute-start | bytes 1179656 | tf_op jit(solution)/shard_map/ppermute | solution.py:32
  105.5 25.3 %collective-permute-start.25 = (bf16[1,1536,128]{2,1,0:T(8,128)(2,1)S(1)}, bf16[1,1536,128]{2,1,0:T(8,128)(2,1)S(1)}, u32[]{:S(2)}, u32[]{:S(2)}) collective-permute-start(bf16[1,1536,128]{2,1,0:T(8,128)(2,1)S(1)} %get-tuple-element.91), channel_id=1, source_target_pairs={{0,16},{8,24},{16,0},{24,8},{32,48},{40,56},{48,32},{56,40},{64,80... | collective-permute-start | bytes 1179656 | tf_op jit(solution)/shard_map/ppermute | solution.py:32
  115.5 20.3 %collective-permute-start.10 = (bf16[1,1536,128]{2,1,0:T(8,128)(2,1)S(1)}, bf16[1,1536,128]{2,1,0:T(8,128)(2,1)S(1)}, u32[]{:S(2)}, u32[]{:S(2)}) collective-permute-start(bf16[1,1536,128]{2,1,0:T(8,128)(2,1)S(1)} %get-tuple-element.76), channel_id=1, source_target_pairs={{0,32},{8,40},{16,48},{24,56},{32,64},{40,72},{48,80},{56,88},{64,... | collective-permute-start | bytes 1179656 | tf_op jit(solution)/shard_map/ppermute | solution.py:32
  115.6 24.4 %collective-permute-start.15 = (bf16[2,1536,128]{2,1,0:T(8,128)(2,1)S(1)}, bf16[2,1536,128]{2,1,0:T(8,128)(2,1)S(1)}, u32[]{:S(2)}, u32[]{:S(2)}) collective-permute-start(bf16[2,1536,128]{2,1,0:T(8,128)(2,1)S(1)} %get-tuple-element.81), channel_id=1, source_target_pairs={{0,8},{8,16},{16,24},{24,0},{32,40},{40,48},{48,56},{56,32},{64,72... | collective-permute-start | bytes 2359304 | tf_op jit(solution)/shard_map/ppermute | solution.py:32
  130.8 26.0 %collective-permute-start.16 = (bf16[2,1536,128]{2,1,0:T(8,128)(2,1)S(1)}, bf16[2,1536,128]{2,1,0:T(8,128)(2,1)S(1)}, u32[]{:S(2)}, u32[]{:S(2)}) collective-permute-start(bf16[2,1536,128]{2,1,0:T(8,128)(2,1)S(1)} %get-tuple-element.82), channel_id=1, source_target_pairs={{0,96},{8,104},{16,112},{24,120},{32,0},{40,8},{48,16},{56,24},{64... | collective-permute-start | bytes 2359304 | tf_op jit(solution)/shard_map/ppermute | solution.py:32
  130.9 30.2 %collective-permute-start.17 = (bf16[2,1536,128]{2,1,0:T(8,128)(2,1)S(1)}, bf16[2,1536,128]{2,1,0:T(8,128)(2,1)S(1)}, u32[]{:S(2)}, u32[]{:S(2)}) collective-permute-start(bf16[2,1536,128]{2,1,0:T(8,128)(2,1)S(1)} %get-tuple-element.83), channel_id=1, source_target_pairs={{0,24},{8,0},{16,8},{24,16},{32,56},{40,32},{48,40},{56,48},{64,88... | collective-permute-start | bytes 2359304 | tf_op jit(solution)/shard_map/ppermute | solution.py:32
  135.8 28.0 %collective-permute-start.18 = (bf16[2,1536,128]{2,1,0:T(8,128)(2,1)S(1)}, bf16[2,1536,128]{2,1,0:T(8,128)(2,1)S(1)}, u32[]{:S(2)}, u32[]{:S(2)}) collective-permute-start(bf16[2,1536,128]{2,1,0:T(8,128)(2,1)S(1)} %get-tuple-element.84), channel_id=1, source_target_pairs={{0,64},{8,72},{16,80},{24,88},{32,96},{40,104},{48,112},{56,120},{... | collective-permute-start | bytes 2359304 | tf_op jit(solution)/shard_map/ppermute | solution.py:32
  136.8 27.0 %collective-permute-start.19 = (bf16[2,1536,128]{2,1,0:T(8,128)(2,1)S(1)}, bf16[2,1536,128]{2,1,0:T(8,128)(2,1)S(1)}, u32[]{:S(2)}, u32[]{:S(2)}) collective-permute-start(bf16[2,1536,128]{2,1,0:T(8,128)(2,1)S(1)} %get-tuple-element.85), channel_id=1, source_target_pairs={{0,16},{8,24},{16,0},{24,8},{32,48},{40,56},{48,32},{56,40},{64,80... | collective-permute-start | bytes 2359304 | tf_op jit(solution)/shard_map/ppermute | solution.py:32
  140.0 29.8 %collective-permute-start.11 = (bf16[1,1536,128]{2,1,0:T(8,128)(2,1)S(1)}, bf16[1,1536,128]{2,1,0:T(8,128)(2,1)S(1)}, u32[]{:S(2)}, u32[]{:S(2)}) collective-permute-start(bf16[1,1536,128]{2,1,0:T(8,128)(2,1)S(1)} %get-tuple-element.77), channel_id=1, source_target_pairs={{0,8},{8,16},{16,24},{24,0},{32,40},{40,48},{48,56},{56,32},{64,72... | collective-permute-start | bytes 1179656 | tf_op jit(solution)/shard_map/ppermute | solution.py:32
  156.8 16.3 %collective-permute-start.12 = (bf16[1,1536,128]{2,1,0:T(8,128)(2,1)S(1)}, bf16[1,1536,128]{2,1,0:T(8,128)(2,1)S(1)}, u32[]{:S(2)}, u32[]{:S(2)}) collective-permute-start(bf16[1,1536,128]{2,1,0:T(8,128)(2,1)S(1)} %get-tuple-element.78), channel_id=1, source_target_pairs={{0,96},{8,104},{16,112},{24,120},{32,0},{40,8},{48,16},{56,24},{64... | collective-permute-start | bytes 1179656 | tf_op jit(solution)/shard_map/ppermute | solution.py:32
  161.0 15.9 %collective-permute-start.13 = (bf16[1,1536,128]{2,1,0:T(8,128)(2,1)S(1)}, bf16[1,1536,128]{2,1,0:T(8,128)(2,1)S(1)}, u32[]{:S(2)}, u32[]{:S(2)}) collective-permute-start(bf16[1,1536,128]{2,1,0:T(8,128)(2,1)S(1)} %get-tuple-element.79), channel_id=1, source_target_pairs={{0,24},{8,0},{16,8},{24,16},{32,56},{40,32},{48,40},{56,48},{64,88... | collective-permute-start | bytes 1179656 | tf_op jit(solution)/shard_map/ppermute | solution.py:32
  163.8 14.5 %collective-permute-start.9 = (bf16[1,1536,128]{2,1,0:T(8,128)(2,1)S(1)}, bf16[1,1536,128]{2,1,0:T(8,128)(2,1)S(1)}, u32[]{:S(2)}, u32[]{:S(2)}) collective-permute-start(bf16[1,1536,128]{2,1,0:T(8,128)(2,1)S(1)} %get-tuple-element.75), channel_id=1, source_target_pairs={{0,16},{8,24},{16,0},{24,8},{32,48},{40,56},{48,32},{56,40},{64,80... | collective-permute-start | bytes 1179656 | tf_op jit(solution)/shard_map/ppermute | solution.py:32
  (2 other events, 25.5 us)
